TPU v7x, 8 devices: a whole 2x2x1 slice. The times are simulated.
8 devices in a mesh: dp: 1 (over z), tpy: 2 (over y), tpx: 4 (over x, core).
Axes of the slice: x: 2, y: 2, z: 1, core: 2. Of those that a mesh axis runs over, the one named last changes fastest.
Arguments:
- embeds: bfloat16 [3, 128, 4096], P(None, 'dp', 'tpy')
- start_pos: int32 [128], P('dp')
- k_cache: bfloat16 [2, 128, 64, 32, 128], P(None, ('dp', 'tpy'), None, 'tpx')
- v_cache: bfloat16 [2, 128, 64, 32, 128], P(None, ('dp', 'tpy'), None, 'tpx')
- w_query: bfloat16 [2, 4096, 4096], P(None, 'tpy', 'tpx')
- w_key: bfloat16 [2, 4096, 4096], P(None, 'tpy', 'tpx')
- w_value: bfloat16 [2, 4096, 4096], P(None, 'tpy', 'tpx')
- w_out: bfloat16 [2, 4096, 4096], P(None, 'tpx', 'tpy')
- w_gate: bfloat16 [2, 4096, 11008], P(None, 'tpy', 'tpx')
- w_up: bfloat16 [2, 4096, 11008], P(None, 'tpy', 'tpx')
- w_down: bfloat16 [2, 11008, 4096], P(None, 'tpx', 'tpy')
- q_gain: bfloat16 [2, 4096], P(None, 'tpx')
- k_gain: bfloat16 [2, 4096], P(None, 'tpx')
- attn_gain: bfloat16 [2, 4096], P(None, 'tpy')
- mlp_gain: bfloat16 [2, 4096], P(None, 'tpy')
Outputs:
- output 1: bfloat16 [3, 128, 4096], P(None, 'dp', 'tpy')
- output 2: bfloat16 [2, 128, 64, 32, 128], P(None, ('dp', 'tpy'), None, 'tpx')
- output 3: bfloat16 [2, 128, 64, 32, 128], P(None, ('dp', 'tpy'), None, 'tpx')
All inputs are finite; a program needn't handle non-finite values.
Results may differ from a plain program's by a relative error of at most 0.02.
Values are sent between devices in bfloat16 or wider.
A program may use at most 1 GiB of HBM per device.

v0:
```python
import math
import jax
import jax.numpy as jnp
from jax import lax
from jax.sharding import PartitionSpec as P

HEAD_DIM = 128
EPS = 1e-6
THETA = 500000.0
SCORE_SCALE = 1.0 / math.sqrt(HEAD_DIM)
NEG_BIG = -1e30


def rms_scale(sq_sum, width):
    return lax.rsqrt(sq_sum / width + EPS)[..., None]


def rope_rotate(values, positions):
    half_dim = HEAD_DIM // 2
    inv_freq = jnp.power(THETA, jnp.arange(half_dim, dtype=jnp.float32) * (-2.0 / HEAD_DIM))
    angles = positions.astype(jnp.float32)[..., None] * inv_freq
    cos_part = jnp.cos(angles)[..., None, :]
    sin_part = jnp.sin(angles)[..., None, :]
    first_half = values[..., :half_dim]
    second_half = values[..., half_dim:]
    return jnp.concatenate([first_half * cos_part - second_half * sin_part, second_half * cos_part + first_half * sin_part], axis=-1)


def attend(q_rot, k_rot, v_new, k_layer, v_layer, start_local):
    num_steps = q_rot.shape[0]
    local_rows = q_rot.shape[1]
    q_heads = q_rot.shape[2]
    kv_heads = k_rot.shape[2]
    seq_len = k_layer.shape[1]
    q_grp = q_rot.reshape(num_steps, local_rows, kv_heads, q_heads // kv_heads, HEAD_DIM)
    old_scores = jnp.einsum('tbkgd,bskd->bktgs', q_grp, k_layer, preferred_element_type=jnp.float32) * SCORE_SCALE
    new_scores = jnp.einsum('tbkgd,ubkd->bktgu', q_grp, k_rot, preferred_element_type=jnp.float32) * SCORE_SCALE
    old_seen = (jnp.arange(seq_len)[None, :] < start_local[:, None])[:, None, None, None, :]
    new_seen = (jnp.arange(num_steps)[None, :] <= jnp.arange(num_steps)[:, None])[None, None, :, None, :]
    joint = jnp.concatenate([jnp.where(old_seen, old_scores, NEG_BIG), jnp.where(new_seen, new_scores, NEG_BIG)], axis=-1)
    attn_probs = jax.nn.softmax(joint, axis=-1).astype(jnp.bfloat16)
    attn_mix = jnp.einsum('bktgs,bskd->bktgd', attn_probs[..., :seq_len], v_layer, preferred_element_type=jnp.float32)
    attn_mix = attn_mix + jnp.einsum('bktgu,ubkd->bktgd', attn_probs[..., seq_len:], v_new, preferred_element_type=jnp.float32)
    return attn_mix.astype(jnp.bfloat16).transpose(2, 0, 1, 3, 4).reshape(num_steps, local_rows, q_heads * HEAD_DIM)


def write_cache(cache, fresh_rows, start_local):
    offset = jnp.arange(cache.shape[2])[None, :] - start_local[:, None]
    result = cache
    for step_idx in range(fresh_rows.shape[1]):
        slot_hit = (offset == step_idx)[None, :, :, None, None]
        result = jnp.where(slot_hit, fresh_rows[:, step_idx][:, :, None], result)
    return result


def solution(mesh):
    tpy_size = mesh.shape['tpy']
    tpx_size = mesh.shape['tpx']
    act_spec = P(None, 'dp', 'tpy')
    cache_spec = P(None, ('dp', 'tpy'), None, 'tpx', None)
    col_spec = P(None, 'tpy', 'tpx')
    row_spec = P(None, 'tpx', 'tpy')
    head_gain = P(None, 'tpx')
    width_gain = P(None, 'tpy')

    def device_fn(embeds, start_pos, k_cache, v_cache, w_query, w_key, w_value, w_out, w_gate, w_up, w_down, q_gain, k_gain, attn_gain, mlp_gain):
        num_steps = embeds.shape[0]
        local_rows = k_cache.shape[1]
        q_cols = w_query.shape[2]
        kv_cols = w_key.shape[2]
        ff_cols = w_gate.shape[2]
        q_width = q_cols * tpx_size
        kv_width = kv_cols * tpx_size
        model_width = embeds.shape[2] * tpy_size
        start_local = lax.dynamic_slice_in_dim(start_pos, lax.axis_index('tpy') * local_rows, local_rows)
        positions = start_local[None, :] + jnp.arange(num_steps, dtype=jnp.int32)[:, None]
        hidden = embeds
        fresh_keys = []
        fresh_vals = []
        for layer_idx in range(k_cache.shape[0]):
            q_part = jnp.einsum('tbd,dn->tbn', hidden, w_query[layer_idx], preferred_element_type=jnp.float32).astype(jnp.bfloat16)
            k_part = jnp.einsum('tbd,dn->tbn', hidden, w_key[layer_idx], preferred_element_type=jnp.float32).astype(jnp.bfloat16)
            v_part = jnp.einsum('tbd,dn->tbn', hidden, w_value[layer_idx], preferred_element_type=jnp.float32).astype(jnp.bfloat16)
            qkv_rows = lax.psum_scatter(jnp.concatenate([q_part, k_part, v_part], axis=-1), 'tpy', scatter_dimension=1, tiled=True)
            q_raw = qkv_rows[..., :q_cols].astype(jnp.float32)
            k_raw = qkv_rows[..., q_cols:q_cols + kv_cols].astype(jnp.float32)
            v_new = qkv_rows[..., q_cols + kv_cols:].reshape(num_steps, local_rows, kv_cols // HEAD_DIM, HEAD_DIM)
            sq_sums = lax.psum(jnp.stack([jnp.sum(q_raw * q_raw, axis=-1), jnp.sum(k_raw * k_raw, axis=-1)]), 'tpx')
            q_norm = q_raw * rms_scale(sq_sums[0], q_width) * q_gain[layer_idx].astype(jnp.float32)
            k_norm = k_raw * rms_scale(sq_sums[1], kv_width) * k_gain[layer_idx].astype(jnp.float32)
            q_rot = rope_rotate(q_norm.reshape(num_steps, local_rows, q_cols // HEAD_DIM, HEAD_DIM), positions).astype(jnp.bfloat16)
            k_rot = rope_rotate(k_norm.reshape(num_steps, local_rows, kv_cols // HEAD_DIM, HEAD_DIM), positions).astype(jnp.bfloat16)
            attn_mix = attend(q_rot, k_rot, v_new, k_cache[layer_idx], v_cache[layer_idx], start_local)
            mix_rows = lax.all_gather(attn_mix, 'tpy', axis=1, tiled=True)
            attn_out = lax.psum(jnp.einsum('tbn,nd->tbd', mix_rows, w_out[layer_idx], preferred_element_type=jnp.float32).astype(jnp.bfloat16), 'tpx').astype(jnp.float32)
            attn_sq = lax.psum(jnp.sum(attn_out * attn_out, axis=-1), 'tpy')
            middle = (hidden.astype(jnp.float32) + attn_out * rms_scale(attn_sq, model_width) * attn_gain[layer_idx].astype(jnp.float32)).astype(jnp.bfloat16)
            gate_part = jnp.einsum('tbd,df->tbf', middle, w_gate[layer_idx], preferred_element_type=jnp.float32).astype(jnp.bfloat16)
            up_part = jnp.einsum('tbd,df->tbf', middle, w_up[layer_idx], preferred_element_type=jnp.float32).astype(jnp.bfloat16)
            gate_up = lax.psum(jnp.concatenate([gate_part, up_part], axis=-1), 'tpy')
            gated_act = (jax.nn.silu(gate_up[..., :ff_cols].astype(jnp.float32)) * gate_up[..., ff_cols:].astype(jnp.float32)).astype(jnp.bfloat16)
            down_out = lax.psum(jnp.einsum('tbf,fd->tbd', gated_act, w_down[layer_idx], preferred_element_type=jnp.float32).astype(jnp.bfloat16), 'tpx').astype(jnp.float32)
            down_sq = lax.psum(jnp.sum(down_out * down_out, axis=-1), 'tpy')
            hidden = (middle.astype(jnp.float32) + down_out * rms_scale(down_sq, model_width) * mlp_gain[layer_idx].astype(jnp.float32)).astype(jnp.bfloat16)
            fresh_keys.append(k_rot)
            fresh_vals.append(v_new)
        k_out = write_cache(k_cache, jnp.stack(fresh_keys), start_local)
        v_out = write_cache(v_cache, jnp.stack(fresh_vals), start_local)
        return hidden, k_out, v_out

    return jax.shard_map(device_fn, mesh=mesh, in_specs=(act_spec, P('dp'), cache_spec, cache_spec, col_spec, col_spec, col_spec, row_spec, col_spec, col_spec, row_spec, head_gain, head_gain, width_gain, width_gain), out_specs=(act_spec, cache_spec, cache_spec), check_vma=False)
```

profile of v0, /device:TPU:0, one launch (start us, length us, event | category | flops | bytes accessed | tf_op | source)
XLA Modules:
  0.0 649.8 jit_solution(10165113249543344210)
XLA Ops:
  7.2 4.6 fusion.104
  11.9 4.1 fusion.107
  22.7 11.7 %fusion.187 = (bf16[1,64,64,8,128]{4,3,2,1,0:T(8,128)(2,1)}, bf16[1,64,64,8,128]{4,3,2,1,0:T(8,128)(2,1)}) fusion(bf16[2,64,64,8,128]{4,3,2,1,0:T(8,128)(2,1)} %param.17), kind=kLoop, calls=%fused_computation.251 | loop fusion | bytes 33554432 | tf_op jit(solution)/shard_map/slice | solution.py:93
  34.5 11.7 %fusion.188 = (bf16[1,64,64,8,128]{4,3,2,1,0:T(8,128)(2,1)}, bf16[1,64,64,8,128]{4,3,2,1,0:T(8,128)(2,1)}) fusion(bf16[2,64,64,8,128]{4,3,2,1,0:T(8,128)(2,1)} %param.18), kind=kLoop, calls=%fused_computation.252 | loop fusion | bytes 33554432 | tf_op jit(solution)/shard_map/slice | solution.py:93
  46.2 8.2 %reduce-scatter.3.cloned.1.call-done = bf16[3,64,3072]{2,1,0:T(8,128)(2,1)} async-done(((bf16[3,128,3072]{2,1,0:T(8,128)(2,1)}), bf16[3,64,3072]{2,1,0:T(8,128)(2,1)}) %reduce-scatter.3.cloned.1.call-update) | async-done | bytes 1179664 | tf_op jit(solution)/shard_map/reduce_scatter | solution.py:84
  55.7 6.6 %psum.84 = f32[2,3,64]{2,1,0:T(4,128)S(1)} all-reduce(f32[2,3,64]{2,1,0:T(4,128)S(1)} %pad_maximum_fusion.6), channel_id=1, replica_groups=mesh['dp'=1,'tpy'=2,'tpx'=4] {'tpx'}, use_global_device_ids=true, to_apply=%region_3.0 | all-reduce | flops 384 | bytes 3072 | tf_op jit(solution)/shard_map/psum | solution.py:88
  68.3 4.7 fusion.194
  83.0 10.9 %all_gather.6 = bf16[3,128,1024]{2,1,0:T(8,128)(2,1)S(1)} all-gather(bf16[3,64,1024]{2,1,0:T(8,128)(2,1)S(1)} %reshape.535), channel_id=1, replica_groups=mesh['dp'=1,'tpy'=2,'tpx'=4] {'tpy'}, dimensions={1}, use_global_device_ids=true | all-gather | bytes 1179648 | tf_op jit(solution)/shard_map/all_gather | solution.py:94
  93.9 5.1 fusion.90
  99.7 36.8 %all-reduce.7.cloned.1.call-done = bf16[3,128,2048]{2,1,0:T(8,128)(2,1)} async-done(((bf16[3,128,2048]{2,1,0:T(8,128)(2,1)}), bf16[3,128,2048]{2,1,0:T(8,128)(2,1)}) %all-reduce.7.cloned.1.call-update) | async-done | bytes 1572880 | tf_op jit(solution)/shard_map/psum | solution.py:95
  138.3 4.9 psum.86
  145.5 9.1 %fusion.35 = bf16[3,128,2752]{1,2,0:T(8,128)(2,1)S(1)} fusion(bf16[3,128,2048]{2,1,0:T(8,128)(2,1)S(1)} %fusion.71, bf16[2,2048,2752]{1,2,0:T(8,128)(2,1)} %param.24), kind=kOutput, calls=%fused_computation.45 | convolution fusion | flops 4329578496 | bytes 14958592 | tf_op jit(solution)/shard_map/tbd,df->tbf/dot_general | solution.py:99
  154.5 8.9 %fusion.32 = bf16[3,128,2752]{1,2,0:T(8,128)(2,1)S(1)} fusion(bf16[3,128,2048]{2,1,0:T(8,128)(2,1)S(1)} %fusion.71, bf16[2,2048,2752]{1,2,0:T(8,128)(2,1)} %param.23), kind=kOutput, calls=%fused_computation.44 | convolution fusion | flops 4329578496 | bytes 14958592 | tf_op jit(solution)/shard_map/tbd,df->tbf/dot_general | solution.py:98
  165.8 102.9 %all-reduce.9.cloned.1.call-done = bf16[3,128,5504]{1,2,0:T(8,128)(2,1)} async-done(((bf16[3,128,5504]{1,2,0:T(8,128)(2,1)}), bf16[3,128,5504]{1,2,0:T(8,128)(2,1)}) %all-reduce.9.cloned.1.call-update) | async-done | bytes 4227088 | tf_op jit(solution)/shard_map/psum | solution.py:100
  268.7 11.8 %fusion.84 = bf16[3,128,2048]{2,1,0:T(8,128)(2,1)} fusion(bf16[2,2752,2048]{2,1,0:T(8,128)(2,1)} %param.25, bf16[3,128,5504]{1,2,0:T(8,128)(2,1)} %all-reduce.9.cloned.1.call-done), kind=kOutput, calls=%fused_computation.96 | convolution fusion | flops 4337762304 | bytes 17072128 | tf_op jit(solution)/shard_map/tbf,fd->tbd/dot_general | solution.py:102
  281.2 36.8 %all-reduce.11.cloned.1.call-done = bf16[3,128,2048]{2,1,0:T(8,128)(2,1)} async-done(((bf16[3,128,2048]{2,1,0:T(8,128)(2,1)}), bf16[3,128,2048]{2,1,0:T(8,128)(2,1)}) %all-reduce.11.cloned.1.call-update) | async-done | bytes 1572880 | tf_op jit(solution)/shard_map/psum | solution.py:102
  319.8 5.3 psum.89
  327.6 4.1 fusion.119
  337.5 32.0 %reduce-scatter.5.cloned.1.call-done = bf16[3,64,3072]{2,1,0:T(8,128)(2,1)} async-done(((bf16[3,128,3072]{2,1,0:T(8,128)(2,1)}), bf16[3,64,3072]{2,1,0:T(8,128)(2,1)}) %reduce-scatter.5.cloned.1.call-update) | async-done | bytes 1179664 | tf_op jit(solution)/shard_map/reduce_scatter | solution.py:84
  370.9 6.3 psum.90
  383.6 4.7 fusion.196
  397.8 10.9 %all_gather.7 = bf16[3,128,1024]{2,1,0:T(8,128)(2,1)S(1)} all-gather(bf16[3,64,1024]{2,1,0:T(8,128)(2,1)S(1)} %reshape.541), channel_id=1, replica_groups=mesh['dp'=1,'tpy'=2,'tpx'=4] {'tpy'}, dimensions={1}, use_global_device_ids=true | all-gather | bytes 1179648 | tf_op jit(solution)/shard_map/all_gather | solution.py:94
  408.7 5.1 fusion.93
  413.9 37.4 %all-reduce.13.cloned.1.call-done = bf16[3,128,2048]{2,1,0:T(8,128)(2,1)} async-done(((bf16[3,128,2048]{2,1,0:T(8,128)(2,1)}), bf16[3,128,2048]{2,1,0:T(8,128)(2,1)}) %all-reduce.13.cloned.1.call-update) | async-done | bytes 1572880 | tf_op jit(solution)/shard_map/psum | solution.py:95
  453.1 4.9 psum.92
  460.3 8.9 %fusion.41 = bf16[3,128,2752]{1,2,0:T(8,128)(2,1)S(1)} fusion(bf16[3,128,2048]{2,1,0:T(8,128)(2,1)S(1)} %fusion.79, bf16[2,2048,2752]{1,2,0:T(8,128)(2,1)} %param.24), kind=kOutput, calls=%fused_computation.47 | convolution fusion | flops 4329578496 | bytes 14958592 | tf_op jit(solution)/shard_map/tbd,df->tbf/dot_general | solution.py:99
  469.2 8.9 %fusion.38 = bf16[3,128,2752]{1,2,0:T(8,128)(2,1)S(1)} fusion(bf16[3,128,2048]{2,1,0:T(8,128)(2,1)S(1)} %fusion.79, bf16[2,2048,2752]{1,2,0:T(8,128)(2,1)} %param.23), kind=kOutput, calls=%fused_computation.46 | convolution fusion | flops 4329578496 | bytes 14958592 | tf_op jit(solution)/shard_map/tbd,df->tbf/dot_general | solution.py:98
  485.7 97.7 %all-reduce.15.cloned.1.call-done = bf16[3,128,5504]{1,2,0:T(8,128)(2,1)} async-done(((bf16[3,128,5504]{1,2,0:T(8,128)(2,1)}), bf16[3,128,5504]{1,2,0:T(8,128)(2,1)}) %all-reduce.15.cloned.1.call-update) | async-done | bytes 4227088 | tf_op jit(solution)/shard_map/psum | solution.py:100
  583.4 11.8 %fusion.87 = bf16[3,128,2048]{2,1,0:T(8,128)(2,1)} fusion(bf16[2,2752,2048]{2,1,0:T(8,128)(2,1)} %param.25, bf16[3,128,5504]{1,2,0:T(8,128)(2,1)} %all-reduce.15.cloned.1.call-done), kind=kOutput, calls=%fused_computation.97 | convolution fusion | flops 4337762304 | bytes 17072128 | tf_op jit(solution)/shard_map/tbf,fd->tbd/dot_general | solution.py:102
  595.2 22.9 %select_select_fusion = (bf16[2,64,64,8,128]{4,3,2,1,0:T(8,128)(2,1)}, bf16[2,64,64,8,128]{4,3,2,1,0:T(8,128)(2,1)}) fusion(bf16[2,64,64,8,128]{4,3,2,1,0:T(8,128)(2,1)} %param.18, pred[64,64]{1,0:T(8,128)(4,1)S(1)} %get-tuple-element.58, pred[64,64]{1,0:T(8,128)(4,1)S(1)} %copy-done.15, pred[64,64]{1,0:T(8,128)(4,1)S(1)} %get-tuple-element.57, ...), kind=kLoop, calls=%fused_computation | loop fusion | flops 50331648 | bytes 68694016 | tf_op jit(solution)/shard_map/jit(_where)/select_n | solution.py:52
  618.2 14.5 %all-reduce.17.cloned.1.call-done = bf16[3,128,2048]{2,1,0:T(8,128)(2,1)} async-done(((bf16[3,128,2048]{2,1,0:T(8,128)(2,1)}), bf16[3,128,2048]{2,1,0:T(8,128)(2,1)}) %all-reduce.17.cloned.1.call-update) | async-done | bytes 1572880 | tf_op jit(solution)/shard_map/psum | solution.py:102
  634.4 4.9 psum.95
  (181 shorter events, 75.1 us)
Async XLA Ops:
  7.2 47.2 %reduce-scatter.3.cloned.1.call-start = ((), (), s32[]{:S(2)}) async-start(), calls=%async_computation.2 | async-start | bytes 3538944 | tf_op jit(solution)/shard_map/reduce_scatter | solution.py:84
  7.2 8.8 %slice-start.8 = ((s8[8388608]{0:T(1024)(128)(4,1)}), s8[4194304]{0:T(1024)(128)(4,1)S(1)}, s32[]{:S(2)}) async-start(s8[8388608]{0:T(1024)(128)(4,1)} %bitcast.272), calls=%async_computation.18 | async-start | bytes 8388608
  19.5 117.0 %all-reduce.7.cloned.1.call-start = ((), (), s32[]{:S(2)}) async-start(), calls=%async_computation.3 | async-start | bytes 3145728 | tf_op jit(solution)/shard_map/psum | solution.py:95
  19.6 53.4 %copy-start.26 = (pred[3,3]{1,0:T(4,128)(4,1)}, pred[3,3]{1,0:T(4,128)(4,1)S(1)}, u32[]{:S(2)}) copy-start(pred[3,3]{1,0:T(4,128)(4,1)S(1)} %iota_compare_fusion.1) | copy-start | bytes 31
  21.6 46.7 %copy-start.23 = (pred[64,64]{1,0:T(8,128)(4,1)}, pred[64,64]{1,0:T(8,128)(4,1)S(1)}, u32[]{:S(2)}) copy-start(pred[64,64]{1,0:T(8,128)(4,1)S(1)} %get-tuple-element.60) | copy-start | bytes 12292
  22.7 43.1 %copy-start.11 = (f32[3,64,64]{2,0,1:T(4,128)}, f32[3,64,64]{2,0,1:T(4,128)S(1)}, u32[]{:S(2)}) copy-start(f32[3,64,64]{2,0,1:T(4,128)S(1)} %get-tuple-element.41) | copy-start | bytes 147460
  22.7 43.1 %copy-start.13 = (f32[3,64,64]{2,0,1:T(4,128)}, f32[3,64,64]{2,0,1:T(4,128)S(1)}, u32[]{:S(2)}) copy-start(f32[3,64,64]{2,0,1:T(4,128)S(1)} %get-tuple-element.42) | copy-start | bytes 147460
  63.4 4.8 slice-start.6
  68.3 4.8 copy-start
  68.3 11.3 %slice-start.2 = ((s8[8388608]{0:T(1024)(128)(4,1)}), s8[4194304]{0:T(1024)(128)(4,1)S(1)}, s32[]{:S(2)}) async-start(s8[8388608]{0:T(1024)(128)(4,1)} %bitcast.225), calls=%async_computation.12 | async-start | bytes 8388608
  73.1 6.5 %slice-start.3 = ((s8[8388608]{0:T(1024)(128)(4,1)}), s8[4194304]{0:T(1024)(128)(4,1)S(1)}, s32[]{:S(2)}) async-start(s8[8388608]{0:T(1024)(128)(4,1)} %bitcast.225), calls=%async_computation.13 | async-start | bytes 8388608
  93.9 5.2 copy-start.17
  99.0 44.2 %copy-start.10 = (bf16[3,128,2048]{2,1,0:T(8,128)(2,1)S(1)}, bf16[3,128,2048]{2,1,0:T(8,128)(2,1)}, u32[]{:S(2)}) copy-start(bf16[3,128,2048]{2,1,0:T(8,128)(2,1)} %param.15) | copy-start | bytes 4718596
  99.1 169.6 %all-reduce.9.cloned.1.call-start = ((), (), s32[]{:S(2)}) async-start(), calls=%async_computation.4 | async-start | bytes 8454144 | tf_op jit(solution)/shard_map/psum | solution.py:100
  165.8 114.8 %copy-start.18 = (bf16[2,2048]{1,0:T(2,128)(2,1)S(1)}, bf16[2,2048]{1,0:T(2,128)(2,1)}, u32[]{:S(2)}) copy-start(bf16[2,2048]{1,0:T(2,128)(2,1)} %param.29) | copy-start | bytes 24580
  165.8 152.2 %all-reduce.11.cloned.1.call-start = ((), (), s32[]{:S(2)}) async-start(), calls=%async_computation.5 | async-start | bytes 3145728 | tf_op jit(solution)/shard_map/psum | solution.py:102
  280.6 89.0 %reduce-scatter.5.cloned.1.call-start = ((), (), s32[]{:S(2)}) async-start(), calls=%async_computation.6 | async-start | bytes 3538944 | tf_op jit(solution)/shard_map/reduce_scatter | solution.py:84
  325.1 6.6 %slice-start.10 = ((s8[8388608]{0:T(1024)(128)(4,1)}), s8[4194304]{0:T(1024)(128)(4,1)S(1)}, s32[]{:S(2)}) async-start(s8[8388608]{0:T(1024)(128)(4,1)} %bitcast.274), calls=%async_computation.20 | async-start | bytes 8388608
  327.6 6.0 slice-start.12
  337.5 40.9 %copy-start.19 = (f32[1,1024]{1,0:T(1,128)S(1)}, f32[1,1024]{1,0:T(1,128)}, u32[]{:S(2)}) copy-start(f32[1,1024]{1,0:T(1,128)} %get-tuple-element.56) | copy-start | bytes 12292
  337.5 40.9 %copy-start.20 = (f32[1,1024]{1,0:T(1,128)S(1)}, f32[1,1024]{1,0:T(1,128)}, u32[]{:S(2)}) copy-start(f32[1,1024]{1,0:T(1,128)} %get-tuple-element.51) | copy-start | bytes 12292
  337.5 113.8 %all-reduce.13.cloned.1.call-start = ((), (), s32[]{:S(2)}) async-start(), calls=%async_computation.7 | async-start | bytes 3145728 | tf_op jit(solution)/shard_map/psum | solution.py:95
  378.3 18.4 %copy-start.7 = (bf16[24,8,8,128]{3,2,1,0:T(8,128)(2,1)}, bf16[24,8,8,128]{3,2,1,0:T(8,128)(2,1)S(1)}, u32[]{:S(2)}) copy-start(bf16[24,8,8,128]{3,2,1,0:T(8,128)(2,1)S(1)} %copy.64) | copy-start | bytes 1179652
  378.4 5.1 slice-start.4
  383.5 4.8 copy-start.4
  383.5 4.8 copy-start.6
  383.5 10.9 %slice-start = ((s8[8388608]{0:T(1024)(128)(4,1)}), s8[4194304]{0:T(1024)(128)(4,1)S(1)}, s32[]{:S(2)}) async-start(s8[8388608]{0:T(1024)(128)(4,1)} %bitcast.223), calls=%async_computation.10 | async-start | bytes 8388608
  388.3 6.1 slice-start.1
  413.9 169.5 %all-reduce.15.cloned.1.call-start = ((), (), s32[]{:S(2)}) async-start(), calls=%async_computation.8 | async-start | bytes 8454144 | tf_op jit(solution)/shard_map/psum | solution.py:100
  480.4 152.2 %all-reduce.17.cloned.1.call-start = ((), (), s32[]{:S(2)}) async-start(), calls=%async_computation.9 | async-start | bytes 3145728 | tf_op jit(solution)/shard_map/psum | solution.py:102
  485.6 109.6 %copy-start.15 = (pred[64,64]{1,0:T(8,128)(4,1)S(1)}, pred[64,64]{1,0:T(8,128)(4,1)}, u32[]{:S(2)}) copy-start(pred[64,64]{1,0:T(8,128)(4,1)} %get-tuple-element.59) | copy-start | bytes 12292
  595.2 44.2 %copy-start.16 = (f32[1,2048]{1,0:T(1,128)S(1)}, f32[1,2048]{1,0:T(1,128)}, u32[]{:S(2)}) copy-start(f32[1,2048]{1,0:T(1,128)} %get-tuple-element.45) | copy-start | bytes 24580
  (18 other events, 49.4 us)
Sparse Core Ops, SparseCore 0:
  19.6 34.7 reduce-scatter.2
  99.2 37.2 all-reduce.6
  165.9 102.7 all-reduce.8
  280.7 37.2 all-reduce.10
  337.6 31.9 reduce-scatter.4
  414.0 37.2 all-reduce.12
  480.6 102.7 all-reduce.14
  595.3 37.2 all-reduce.16
where the time goes:
time: 656 us; the launch traced here: 650 us
  waiting for transfers between devices  366 us (56%)
  matrix products  108 us (16%)
  other arithmetic  74 us (11%)
  blocking collectives  54.8 us (8%)
  local copies, waits for them, and re-layouts  31.1 us (5%)
  between operations  15.3 us (2%)
    psum x2, waiting for transfers between devices, device_fn(): gate_up = lax.psum(jnp.concatenate([gate_part, up_part], axis=-1), 'tpy')  201 us
    psum x2, waiting for transfers between devices, device_fn(): lax.psum(jnp.einsum('tbn,nd->tbd', mix_rows, w_out[layer_idx], preferred_...  74.2 us
    psum x2, waiting for transfers between devices, device_fn(): lax.psum(jnp.einsum('tbf,fd->tbd', gated_act, w_down[layer_idx], preferre...  51.3 us
    reduce_scatter x2, waiting for transfers between devices, device_fn(): lax.psum_scatter(jnp.concatenate([q_part, k_part, v_part], axis=-1), 'tpy...  40.2 us
    dot_general x2, matrix products, device_fn(): jnp.einsum('tbf,fd->tbd', gated_act, w_down[layer_idx], preferred_element...  23.7 us
    select_n x1, other arithmetic, write_cache(): result = jnp.where(slot_hit, fresh_rows[:, step_idx][:, :, None], result)  22.9 us
    all_gather x2, blocking collectives, device_fn(): mix_rows = lax.all_gather(attn_mix, 'tpy', axis=1, tiled=True)  21.8 us
    dot_general x2, matrix products, device_fn(): jnp.einsum('tbd,df->tbf', middle, w_up[layer_idx], preferred_element_type...  18 us
  transfers between devices with their start and end apart: 8, of which 8 were waited for; matrix products, arithmetic and copies ran while one was open for 8% of the time, Pallas kernels for 0%

commit v1 on v0

v1 whole, which is shorter than its diff:
```python
import functools
import math
import jax
import jax.numpy as jnp
from jax import lax
from jax.experimental import pallas as pl
from jax.experimental.pallas import tpu as pltpu
from jax.sharding import PartitionSpec as P

HEAD_DIM = 128
EPS = 1e-6
THETA = 500000.0
SCORE_SCALE = 1.0 / math.sqrt(HEAD_DIM)
NEG_BIG = -1e30
MESH = pl.DeviceIdType.MESH
BF = jnp.bfloat16
F32 = jnp.float32

L = 2
T = 3
NB = 2
RB = 32
R = T * RB
HL = 8
DW = 2048
QW = HL * HEAD_DIM
FW = 2752
FP = 2816
SEQ = 64
SH = SEQ * HL
CB = 4
NCH = RB // CB
TW = 512
HALF = DW // 2
GU_TILES = [(0, 512), (512, 512), (1024, 512), (1536, 512), (2048, 512), (2560, 256)]
QKV_TILES = [(0, 0), (0, 512), (0, 1024), (0, 1536), (1, 0), (1, 512)]


def dot(a, b):
    return jnp.dot(a, b, preferred_element_type=F32)


def dot_t(a, b):
    return lax.dot_general(a, b, (((1,), (1,)), ((), ())), preferred_element_type=F32)


def main_kernel(start_ref, emb_ref, kc_ref, vc_ref, wq_ref, wk_ref, wv_ref, wo_ref, wg_ref, wu_ref, wd_ref,
                qg_ref, kg_ref, ag_ref, mg_ref, cos_ref, sin_ref,
                y_ref, kn_ref, vn_ref,
                X, W1, WO, WD, GP, GR, C, OB, QS, KS, VS, OS, KO, VO, KB, VB, XP, XC, XS, XR, AF, RSUM, RSC, ST, SR,
                in_sem, q_wsem, g_wsem, o_wsem, d_wsem, kv_sem, ko_sem, y_sem,
                g_ss, g_rs, c_ss, c_rs, o_ss, o_rs, p_ss, p_rs, x_ss, x_rs, a_ss, a_rs, st_ss, st_rs):
    ty = lax.axis_index("tpy")
    tx = lax.axis_index("tpx")
    core = lax.rem(tx, 2)
    oy = 1 - ty
    cx = tx + 1 - 2 * core
    xx = lax.rem(tx + 2, 4)
    dx = 3 - tx
    ypeer = {"tpy": oy}
    cpeer = {"tpx": cx}
    xpeer = {"tpx": xx}
    xdiag = {"tpx": dx}
    ydiag = {"tpy": oy, "tpx": cx}
    own_half = pl.ds(pl.multiple_of(core * HALF, HALF), HALF)
    oth_half = pl.ds(pl.multiple_of((1 - core) * HALF, HALF), HALF)

    def rc(src, dst, ss, rs, dev):
        return pltpu.make_async_remote_copy(src_ref=src, dst_ref=dst, send_sem=ss, recv_sem=rs, device_id=dev, device_id_type=MESH)

    def lc(src, dst, sem):
        return pltpu.make_async_copy(src, dst, sem)

    def emb_copies():
        out = []
        for m in range(NB):
            for y in range(2):
                for t in range(T):
                    out.append(lc(emb_ref.at[t, pl.ds(y * NB * RB + m * RB, RB)], X.at[m, y, pl.ds(t * RB, RB)], in_sem.at[(m * 2 + y) * T + t]))
        return out

    def qkv_load(l, n):
        j, c0 = QKV_TILES[n]
        src = (wq_ref, wk_ref, wv_ref)[n // 2]
        return lc(src.at[l, :, pl.ds((n % 2) * TW, TW)], W1.at[j, :, pl.ds(c0, TW)], q_wsem.at[n])

    def qkv_loads(l):
        return [qkv_load(l, n) for n in range(6)]

    def gu_loads(l):
        return [lc((wg_ref, wu_ref)[j].at[l, pl.ds(r * 512, 512)], W1.at[j, pl.ds(r * 512, 512)], g_wsem.at[j * 4 + r]) for r in range(4) for j in range(2)]

    def wo_loads(l):
        return [lc(wo_ref.at[l], WO, o_wsem.at[0])]

    def wd_loads(l):
        return [lc(wd_ref.at[l, pl.ds(r * 688, 688)], WD.at[pl.ds(r * 688, 688)], d_wsem.at[r]) for r in range(4)]

    def start(copies):
        for cp in copies:
            cp.start()

    def wait(copies):
        for cp in copies:
            cp.wait()

    def kv_copies(l, m, c, slot):
        rows = pl.ds(m * RB + c * CB, CB)
        return [lc(kc_ref.at[l, rows], KB.at[slot], kv_sem.at[0, slot]), lc(vc_ref.at[l, rows], VB.at[slot], kv_sem.at[1, slot])]

    start(emb_copies())
    start(qkv_loads(0))

    barrier = pltpu.get_barrier_semaphore()
    for dev in (ypeer, cpeer, xpeer, xdiag, ydiag):
        pl.semaphore_signal(barrier, inc=1, device_id=dev, device_id_type=MESH)
    pl.semaphore_wait(barrier, 5)

    start(kv_copies(0, 0, 0, 0))
    start(kv_copies(0, 0, 1, 1))
    start(wo_loads(0))
    start(wd_loads(0))

    def tile_copy(m, j, n, c0, w):
        return rc(GP.at[m, j, oy, :, pl.ds(c0, w)], GR.at[m, j, :, pl.ds(c0, w)], g_ss.at[m, j, n], g_rs.at[m, j, n], ypeer)

    def compute_tile(m, j, c0, w):
        xm = X[m].reshape(2 * R, DW)
        res = dot(xm, W1[j, :, pl.ds(c0, w)]).astype(BF)
        GP[m, j, :, :, pl.ds(c0, w)] = res.reshape(2, R, w)

    def phase_q(m, l, first):
        for j, cnt in ((0, 4), (1, 2)):
            if first:
                for i in range(cnt):
                    qkv_load(l, j * 4 + i).wait()
                    compute_tile(m, j, i * TW, TW)
                    tile_copy(m, j, i, i * TW, TW).start()
            else:
                def body(i, _):
                    c0 = pl.multiple_of(i * TW, TW)
                    compute_tile(m, j, c0, TW)
                    tile_copy(m, j, i, c0, TW).start()
                    return 0
                lax.fori_loop(0, cnt, body, 0)

    def phase_g(m, l, send):
        def body(i, _):
            c0 = pl.multiple_of(i * TW, TW)
            for j in range(2):
                compute_tile(m, j, c0, TW)
                if send:
                    tile_copy(m, j, i, c0, TW).start()
            return 0
        lax.fori_loop(0, 5, body, 0)
        for j in range(2):
            compute_tile(m, j, 2560, 192)
            if send:
                tile_copy(m, j, 5, 2560, 256).start()

    def send_g(m):
        for n, (c0, w) in enumerate(GU_TILES):
            for j in range(2):
                tile_copy(m, j, n, c0, w).start()

    def stat_copies(kind, m):
        peers = (cpeer, xpeer, xdiag) if kind == 0 else (cpeer, ypeer, ydiag)
        return [rc(ST.at[kind, m], SR.at[kind, m, k], st_ss.at[kind, m, k], st_rs.at[kind, m, k], peers[k]) for k in range(3)]

    def stat_send(kind, m):
        v0 = jnp.sum(RSUM[0], axis=1, keepdims=True)
        v1 = jnp.sum(RSUM[1], axis=1, keepdims=True)
        lane = lax.broadcasted_iota(jnp.int32, (R, 128), 1)
        both = jnp.where(lane == 0, v0, v1)
        full = jnp.concatenate([both, jnp.zeros((128 - R, 128), F32)], axis=0)
        ST[kind, m] = full.T[0:8]
        start(stat_copies(kind, m))

    def stat_recv(kind, m):
        wait(stat_copies(kind, m))
        total = (ST[kind, m] + SR[kind, m, 0]) + (SR[kind, m, 1] + SR[kind, m, 2])
        back = jnp.concatenate([total] * 16, axis=0).T
        scale = lax.rsqrt(back / 4096.0 + EPS)
        RSC[0] = jnp.broadcast_to(scale[0:R, 0:1], (R, 128))
        RSC[1] = jnp.broadcast_to(scale[0:R, 1:2], (R, 128))

    def phase_s(m):
        for n, (j, c0) in enumerate(QKV_TILES):
            tile_copy(m, j, c0 // TW, c0, TW).wait()

        def body(i, _):
            rows = pl.ds(pl.multiple_of(i * 16, 16), 16)
            for j in range(2):
                acc = jnp.zeros((16, 128), F32)
                for h in range(8):
                    cols = pl.ds((j * 8 + h) * 128, 128)
                    z = (GP[m, 0, ty, rows, cols].astype(F32) + GR[m, 0, rows, cols].astype(F32)).astype(BF)
                    GR[m, 0, rows, cols] = z
                    zf = z.astype(F32)
                    acc = acc + zf * zf
                RSUM[j, rows] = acc
            for h in range(8):
                cols = pl.ds(h * 128, 128)
                GR[m, 1, rows, cols] = (GP[m, 1, ty, rows, cols].astype(F32) + GR[m, 1, rows, cols].astype(F32)).astype(BF)
            return 0
        lax.fori_loop(0, R // 16, body, 0)
        stat_send(0, m)

    def phase_t1(m, l):
        stat_recv(0, m)

        def body(i, _):
            rows = pl.ds(pl.multiple_of(i * 16, 16), 16)
            t = i // 2
            dst = pl.ds(pl.multiple_of(lax.rem(i, 2) * 16, 16), 16)
            cosv = cos_ref[m, rows]
            sinv = sin_ref[m, rows]
            for j, (out, gain) in enumerate(((QS, qg_ref), (KS, kg_ref))):
                scale = RSC[j, rows]
                for h in range(8):
                    z = GR[m, 0, rows, pl.ds((j * 8 + h) * 128, 128)].astype(F32)
                    z = z * scale * gain[l, :, pl.ds(h * 128, 128)]
                    rot = z * cosv + pltpu.roll(z, 64, 1) * sinv
                    out[t, dst, h, :] = rot.astype(BF).astype(F32)
            for h in range(8):
                VS[t, dst, h, :] = GR[m, 1, rows, pl.ds(h * 128, 128)].astype(F32)
            return 0
        lax.fori_loop(0, R // 16, body, 0)

    def ko_copies(l, m):
        rows = pl.ds(m * RB, RB)
        return [lc(KO.at[m], kn_ref.at[l, rows], ko_sem.at[0, m]), lc(VO.at[m], vn_ref.at[l, rows], ko_sem.at[1, m])]

    def o_copy(m):
        return rc(OB.at[m, ty], OB.at[m, ty], o_ss.at[m], o_rs.at[m], ypeer)

    def phase_t2(m, l):
        if l > 0:
            wait(ko_copies(l - 1, m))
        row = lax.broadcasted_iota(jnp.int32, (T * HL, SH), 0)
        col = lax.broadcasted_iota(jnp.int32, (T * HL, SH), 1)
        colm = jnp.where(lax.rem(row, HL) == lax.rem(col, HL), col, SH)
        rown = lax.broadcasted_iota(jnp.int32, (T * HL, T * HL), 0)
        coln = lax.broadcasted_iota(jnp.int32, (T * HL, T * HL), 1)
        newm = (lax.rem(rown, HL) == lax.rem(coln, HL)) & (coln <= rown)

        def chunk(c, _):
            slot = lax.rem(c, 2)
            wait(kv_copies(l, m, c, slot))
            for k in range(CB):
                i = c * CB + k
                q = QS[:, i].reshape(T * HL, HEAD_DIM).astype(BF)
                kn = KS[:, i].reshape(T * HL, HEAD_DIM).astype(BF)
                vn = VS[:, i].reshape(T * HL, HEAD_DIM).astype(BF)
                limit = start_ref[m * RB + i] * HL
                s_old = jnp.where(colm < limit, dot_t(q, KB[slot, k]) * SCORE_SCALE, NEG_BIG)
                s_new = jnp.where(newm, dot_t(q, kn) * SCORE_SCALE, NEG_BIG)
                top = jnp.maximum(jnp.max(s_old, axis=1, keepdims=True), jnp.max(s_new, axis=1, keepdims=True))
                e_old = jnp.exp(s_old - top)
                e_new = jnp.exp(s_new - top)
                den = jnp.sum(e_old, axis=1, keepdims=True) + jnp.sum(e_new, axis=1, keepdims=True)
                o = dot((e_old / den).astype(BF), VB[slot, k]) + dot((e_new / den).astype(BF), vn)
                OS[:, i] = o.reshape(T, HL, HEAD_DIM)
                KO[m, i] = kn
                VO[m, i] = vn

            @pl.when(c < NCH - 2)
            def _():
                start(kv_copies(l, m, c + 2, slot))
            return 0
        lax.fori_loop(0, NCH, chunk, 0)
        start(ko_copies(l, m))
        nxt = (l, m + 1) if m + 1 < NB else (l + 1, 0)
        if nxt[0] < L:
            start(kv_copies(nxt[0], nxt[1], 0, 0))
            start(kv_copies(nxt[0], nxt[1], 1, 1))

        def body(i, _):
            rows = pl.ds(pl.multiple_of(i * 16, 16), 16)
            t = i // 2
            src = pl.ds(pl.multiple_of(lax.rem(i, 2) * 16, 16), 16)
            for h in range(8):
                OB[m, ty, rows, pl.ds(h * 128, 128)] = OS[t, src, h, :].astype(BF)
            return 0
        lax.fori_loop(0, R // 16, body, 0)
        o_copy(m).start()

    def p_copy(m):
        return rc(XP.at[m, :, oth_half], XC.at[m], p_ss.at[m], p_rs.at[m], cpeer)

    def x_copy(ph, m):
        return rc(XS.at[m], XR.at[ph, m], x_ss.at[m], x_rs.at[ph, m], xpeer)

    def a_copy(m):
        return rc(AF.at[m, :, own_half], AF.at[m, :, own_half], a_ss.at[m], a_rs.at[m], cpeer)

    def phase_o(m, l):
        o_copy(m).wait()
        for half in (1 - core, core):
            def body(i, _):
                cols = pl.ds(pl.multiple_of(half * HALF + i * TW, TW), TW)
                XP[m, :, cols] = dot(OB[m].reshape(2 * R, QW), WO[:, cols]).astype(BF)
                return 0
            lax.fori_loop(0, 2, body, 0)
            if half is not core:
                p_copy(m).start()

    def phase_d(m, l):
        for n, (c0, w) in enumerate(GU_TILES):
            c_copy(m, n, c0, w).wait()
        for half in (1 - core, core):
            def body(i, _):
                cols = pl.ds(pl.multiple_of(half * HALF + i * TW, TW), TW)
                cm = C[m].reshape(2 * R, FP)
                XP[m, :, cols] = dot(cm[:, :FW], WD[:, cols]).astype(BF)
                return 0
            lax.fori_loop(0, 2, body, 0)
            if half is not core:
                p_copy(m).start()

    def phase_2(ph, m):
        p_copy(m).wait()

        def body(i, _):
            rows = pl.ds(pl.multiple_of(i * 16, 16), 16)
            XS[m, rows] = (XP[m, rows, own_half].astype(F32) + XC[m, rows].astype(F32)).astype(BF)
            return 0
        lax.fori_loop(0, 2 * R // 16, body, 0)
        x_copy(ph, m).start()

    def phase_3(ph, m):
        x_copy(ph, m).wait()

        def body(i, _):
            rows = pl.ds(pl.multiple_of(i * 16, 16), 16)
            z = (XS[m, rows].astype(F32) + XR[ph, m, rows].astype(F32)).astype(BF)
            AF[m, rows, own_half] = z
            zf = z.astype(F32)
            sq = zf * zf
            acc = sq[:, 0:128]
            for h in range(1, 8):
                acc = acc + sq[:, h * 128:(h + 1) * 128]
            RSUM[i // 6, pl.ds(pl.multiple_of(lax.rem(i, 6) * 16, 16), 16)] = acc
            return 0
        lax.fori_loop(0, 2 * R // 16, body, 0)
        a_copy(m).start()
        stat_send(1 + ph, m)

    def phase_h(ph, m, l):
        gain = (ag_ref, mg_ref)[ph]
        stat_recv(1 + ph, m)
        a_copy(m).wait()

        def body(i, _):
            y = i // 6
            rows = pl.ds(pl.multiple_of(lax.rem(i, 6) * 16, 16), 16)
            arow = pl.ds(pl.multiple_of(i * 16, 16), 16)
            scale = RSC[y, rows]
            for h in range(16):
                cols = pl.ds(h * 128, 128)
                X[m, y, rows, cols] = (X[m, y, rows, cols].astype(F32) + AF[m, arow, cols].astype(F32) * scale * gain[l, :, cols]).astype(BF)
            return 0
        lax.fori_loop(0, 2 * R // 16, body, 0)

    def c_copy(m, n, c0, w):
        return rc(C.at[m, ty, :, pl.ds(c0, w)], C.at[m, ty, :, pl.ds(c0, w)], c_ss.at[m, n], c_rs.at[m, n], ypeer)

    def phase_c(m, lo, hi):
        for n in range(lo, hi):
            c0, w = GU_TILES[n]
            for j in range(2):
                tile_copy(m, j, n, c0, w).wait()

            def body(i, _):
                rows = pl.ds(pl.multiple_of(i * 16, 16), 16)
                cols = pl.ds(c0, w)
                g = (GP[m, 0, ty, rows, cols].astype(F32) + GR[m, 0, rows, cols].astype(F32)).astype(BF).astype(F32)
                u = (GP[m, 1, ty, rows, cols].astype(F32) + GR[m, 1, rows, cols].astype(F32)).astype(BF).astype(F32)
                C[m, ty, rows, cols] = (jax.nn.silu(g) * u).astype(BF)
                return 0
            lax.fori_loop(0, R // 16, body, 0)
            c_copy(m, n, c0, w).start()

    def y_copies(m):
        out = []
        for y in range(2):
            for t in range(T):
                out.append(lc(X.at[m, y, pl.ds(t * RB, RB)], y_ref.at[t, pl.ds(y * NB * RB + m * RB, RB)], y_sem.at[(m * 2 + y) * T + t]))
        return out

    A, B = 0, 1
    wait(emb_copies())
    phase_q(A, 0, True)
    phase_q(B, 0, False)
    for l in range(L):
        start(gu_loads(l))
        phase_s(A)
        phase_t1(A, l)
        phase_t2(A, l)
        phase_s(B)
        phase_t1(B, l)
        wait(wo_loads(l))
        phase_o(A, l)
        phase_2(0, A)
        phase_t2(B, l)
        phase_3(0, A)
        phase_o(B, l)
        phase_h(0, A, l)
        phase_2(0, B)
        if l + 1 < L:
            start(wo_loads(l + 1))
        wait(gu_loads(l))
        phase_g(A, l, True)
        phase_3(0, B)
        phase_h(0, B, l)
        phase_g(B, l, False)
        if l + 1 < L:
            start(qkv_loads(l + 1))
        phase_c(A, 0, 6)
        send_g(B)
        wait(wd_loads(l))
        phase_d(A, l)
        phase_2(1, A)
        phase_c(B, 0, 3)
        phase_3(1, A)
        phase_h(1, A, l)
        phase_c(B, 3, 6)
        if l + 1 < L:
            phase_q(A, l + 1, True)
        else:
            start(y_copies(A))
        phase_d(B, l)
        if l + 1 < L:
            start(wd_loads(l + 1))
        phase_2(1, B)
        phase_3(1, B)
        phase_h(1, B, l)
        if l + 1 < L:
            phase_q(B, l + 1, False)
        else:
            start(y_copies(B))
    wait(y_copies(A))
    wait(y_copies(B))
    for m in range(NB):
        wait(ko_copies(L - 1, m))


def cache_kernel(start_ref, k_ref, v_ref, kn_ref, vn_ref, ko_ref, vo_ref):
    c = pl.program_id(1)
    ko_ref[...] = k_ref[...]
    vo_ref[...] = v_ref[...]
    for i in range(k_ref.shape[1]):
        p = start_ref[c * k_ref.shape[1] + i]
        for t in range(T):
            ko_ref[0, i, p + t] = kn_ref[0, i, t]
            vo_ref[0, i, p + t] = vn_ref[0, i, t]


def solution(mesh):
    act_spec = P(None, 'dp', 'tpy')
    cache_spec = P(None, ('dp', 'tpy'), None, 'tpx', None)
    col_spec = P(None, 'tpy', 'tpx')
    row_spec = P(None, 'tpx', 'tpy')
    head_gain = P(None, 'tpx')
    width_gain = P(None, 'tpy')

    def device_fn(embeds, start_pos, k_cache, v_cache, w_query, w_key, w_value, w_out, w_gate, w_up, w_down, q_gain, k_gain, attn_gain, mlp_gain):
        rows = NB * RB
        start_local = lax.dynamic_slice_in_dim(start_pos, lax.axis_index('tpy') * rows, rows)
        pos = (start_local.reshape(NB, 1, RB) + jnp.arange(T, dtype=jnp.int32)[None, :, None]).reshape(NB, R)
        inv_freq = jnp.power(THETA, jnp.arange(HEAD_DIM // 2, dtype=F32) * (-2.0 / HEAD_DIM))
        ang = pos.astype(F32)[..., None] * inv_freq
        cos_part, sin_part = jnp.cos(ang), jnp.sin(ang)
        cos2 = jnp.concatenate([cos_part, cos_part], axis=-1)
        sin2 = jnp.concatenate([-sin_part, sin_part], axis=-1)
        gains = [g.astype(F32).reshape(L, 1, -1) for g in (q_gain, k_gain, attn_gain, mlp_gain)]
        hbm = pl.BlockSpec(memory_space=pl.ANY)
        vm = pl.BlockSpec(memory_space=pltpu.VMEM)
        dma = pltpu.SemaphoreType.DMA
        y, kn, vn = pl.pallas_call(
            main_kernel,
            out_shape=[
                jax.ShapeDtypeStruct(embeds.shape, BF),
                jax.ShapeDtypeStruct((L, rows, T * HL, HEAD_DIM), BF),
                jax.ShapeDtypeStruct((L, rows, T * HL, HEAD_DIM), BF),
            ],
            in_specs=[pl.BlockSpec(memory_space=pltpu.SMEM)] + [hbm] * 10 + [vm] * 6,
            out_specs=[hbm] * 3,
            scratch_shapes=[
                pltpu.VMEM((NB, 2, R, DW), BF),
                pltpu.VMEM((2, DW, FW), BF),
                pltpu.VMEM((QW, DW), BF),
                pltpu.VMEM((FW, DW), BF),
                pltpu.VMEM((NB, 2, 2, R, FP), BF),
                pltpu.VMEM((NB, 2, R, FP), BF),
                pltpu.VMEM((NB, 2, R, FP), BF),
                pltpu.VMEM((NB, 2, R, QW), BF),
                pltpu.VMEM((T, RB, HL, HEAD_DIM), F32),
                pltpu.VMEM((T, RB, HL, HEAD_DIM), F32),
                pltpu.VMEM((T, RB, HL, HEAD_DIM), F32),
                pltpu.VMEM((T, RB, HL, HEAD_DIM), F32),
                pltpu.VMEM((NB, RB, T * HL, HEAD_DIM), BF),
                pltpu.VMEM((NB, RB, T * HL, HEAD_DIM), BF),
                pltpu.VMEM((2, CB, SH, HEAD_DIM), BF),
                pltpu.VMEM((2, CB, SH, HEAD_DIM), BF),
                pltpu.VMEM((NB, 2 * R, DW), BF),
                pltpu.VMEM((NB, 2 * R, HALF), BF),
                pltpu.VMEM((NB, 2 * R, HALF), BF),
                pltpu.VMEM((2, NB, 2 * R, HALF), BF),
                pltpu.VMEM((NB, 2 * R, DW), BF),
                pltpu.VMEM((2, R, 128), F32),
                pltpu.VMEM((2, R, 128), F32),
                pltpu.VMEM((3, NB, 8, 128), F32),
                pltpu.VMEM((3, NB, 3, 8, 128), F32),
                dma((NB * 2 * T,)), dma((6,)), dma((8,)), dma((1,)), dma((4,)), dma((2, 2)), dma((2, NB)), dma((NB * 2 * T,)),
                dma((NB, 2, 6)), dma((NB, 2, 6)), dma((NB, 6)), dma((NB, 6)), dma((NB,)), dma((NB,)),
                dma((NB,)), dma((NB,)), dma((NB,)), dma((2, NB)), dma((NB,)), dma((NB,)), dma((3, NB, 3)), dma((3, NB, 3)),
            ],
            compiler_params=pltpu.CompilerParams(collective_id=0, has_side_effects=True, vmem_limit_bytes=67043328),
            name="layers",
        )(start_local, embeds, k_cache.reshape(L, rows, SH, HEAD_DIM), v_cache.reshape(L, rows, SH, HEAD_DIM),
          w_query, w_key, w_value, w_out, w_gate, w_up, w_down, *gains, cos2, sin2)
        bc = 8
        big = pl.BlockSpec((1, bc, SEQ, HL, HEAD_DIM), lambda l, c, s: (l, c, 0, 0, 0))
        small = pl.BlockSpec((1, bc, T, HL, HEAD_DIM), lambda l, c, s: (l, c, 0, 0, 0))
        k_out, v_out = pl.pallas_call(
            cache_kernel,
            out_shape=[jax.ShapeDtypeStruct(k_cache.shape, BF)] * 2,
            grid_spec=pltpu.PrefetchScalarGridSpec(
                num_scalar_prefetch=1, grid=(L, rows // bc), in_specs=[big, big, small, small], out_specs=[big, big]),
            name="caches",
        )(start_local, k_cache, v_cache, kn.reshape(L, rows, T, HL, HEAD_DIM), vn.reshape(L, rows, T, HL, HEAD_DIM))
        return y, k_out, v_out

    return jax.shard_map(device_fn, mesh=mesh, in_specs=(act_spec, P('dp'), cache_spec, cache_spec, col_spec, col_spec, col_spec, row_spec, col_spec, col_spec, row_spec, head_gain, head_gain, width_gain, width_gain), out_specs=(act_spec, cache_spec, cache_spec), check_vma=False)
```

time: 656 us -> 425 us (0.65)
  waiting for transfers between devices: 366 us -> 0 us
  Pallas kernels: 0 us -> 355 us
  matrix products: 108 us -> 0 us
  other arithmetic: 74 us -> 1.23 us
  blocking collectives: 54.8 us -> 0 us
  local copies, waits for them, and re-layouts: 31.1 us -> 66.4 us
  between operations: 15.3 us -> 0.67 us
    pallas_call x0 -> x2, Pallas kernels: none -> 355 us  [the longest x1 327 us: device_fn(): pl.pallas_call(main_kernel, out_shape=[jax.ShapeDtypeStruct(embeds.shape,...]
    psum x6 -> x0, waiting for transfers between devices: 326 us -> none  [the longest x2 201 us: device_fn(): gate_up = lax.psum(jnp.concatenate([gate_part, up_part], axis=-1), 'tpy')]
    dot_general x22 -> x0, matrix products: 108 us -> none  [the longest x2 23.7 us: device_fn(): jnp.einsum('tbf,fd->tbd', gated_act, w_down[layer_idx], preferred_element...]
    unnamed x94 -> x7, local copies, waits for them, and re-layouts: 2.77 us -> 60.2 us
    reduce_scatter x2 -> x0, waiting for transfers between devices: 40.2 us -> none  [device_fn(): lax.psum_scatter(jnp.concatenate([q_part, k_part, v_part], axis=-1), 'tpy...]
    psum x6 -> x0, blocking collectives: 33 us -> none  [the longest x2 12.9 us: device_fn(): lax.psum(jnp.stack([jnp.sum(q_raw * q_raw, axis=-1), jnp.sum(k_raw * k_ra...]
    slice x8 -> x0, local copies, waits for them, and re-layouts: 27.6 us -> none  [the longest x1 11.7 us: device_fn(): k_cache[layer_idx]]
    select_n x1 -> x0, other arithmetic: 22.9 us -> none  [write_cache(): result = jnp.where(slot_hit, fresh_rows[:, step_idx][:, :, None], result)]
  transfers between devices with their start and end apart: 8 -> 0, of which waited for: 8 -> 0; matrix products, arithmetic and copies ran while one was open for 8% -> 0% of each run, Pallas kernels for 0% -> 0%
where the time goes in v1:
time: 425 us; the launch traced here: 423 us
  Pallas kernels  355 us (84%)
  local copies, waits for them, and re-layouts  66.4 us (16%)
    pallas_call x1, Pallas kernels, device_fn(): pl.pallas_call(main_kernel, out_shape=[jax.ShapeDtypeStruct(embeds.shape,...  327 us
    unnamed x7, local copies, waits for them, and re-layouts  60.2 us
    pallas_call x1, Pallas kernels, device_fn(): pl.pallas_call(cache_kernel, out_shape=[jax.ShapeDtypeStruct(k_cache.shap...  27.9 us

profile of v1, /device:TPU:0, one launch (start us, length us, event | category | flops | bytes accessed | tf_op | source)
XLA Modules:
  0.0 423.1 jit_solution(1461432753724850590)
XLA Ops:
  0.6 0.7 dynamic_slice.3.start_ref
  1.4 0.0 copy-start.1
  1.4 0.6 copy-done.1
  2.0 0.1 add.30
  2.0 0.1 add.34
  2.1 0.1 add.32
  2.2 1.3 reshape.80.qg_ref
  3.5 1.3 reshape.82.kg_ref
  4.8 1.3 reshape.84.ag_ref
  6.1 1.3 reshape.86.mg_ref
  7.4 0.4 fusion
  7.8 0.8 pad_maximum_fusion
  8.6 29.7 %copy.20.wg_ref = bf16[2,2048,2752]{2,1,0:T(8,128)(2,1)} copy(bf16[2,2048,2752]{1,2,0:T(8,128)(2,1)} %param.23) | data formatting | bytes 45088768 | tf_op args[8]
  38.4 28.8 %copy.21.wu_ref = bf16[2,2048,2752]{2,1,0:T(8,128)(2,1)} copy(bf16[2,2048,2752]{1,2,0:T(8,128)(2,1)} %param.24) | data formatting | bytes 45088768 | tf_op args[9]
  67.2 326.9 %layers.1 = (bf16[3,128,2048]{2,1,0:T(8,128)(2,1)}, bf16[2,64,24,128]{3,2,1,0:T(8,128)(2,1)}, bf16[2,64,24,128]{3,2,1,0:T(8,128)(2,1)}) custom-call(s32[64]{0:T(128)} %copy-done.1, bf16[3,128,2048]{2,1,0:T(8,128)(2,1)} %emb_ref.1, bf16[2,64,512,128]{3,2,1,0:T(8,128)(2,1)} %bitcast.4, bf16[2,64,512,128]{3,2,1,0:T(8,128)(2,1)} %bitcast.5, ...), custom_call_target="tpu_custom_call" | custom-call | tf_op jit(solution)/shard_map/layers/pallas_call | solution.py:480
  394.1 0.0 copy-start
  394.1 27.9 %caches.1 = (bf16[2,64,64,8,128]{4,3,2,1,0:T(8,128)(2,1)}, bf16[2,64,64,8,128]{4,3,2,1,0:T(8,128)(2,1)}) custom-call(s32[64]{0:T(128)} %copy-done.1, bf16[2,64,64,8,128]{4,3,2,1,0:T(8,128)(2,1)} %k_ref.1, bf16[2,64,64,8,128]{4,3,2,1,0:T(8,128)(2,1)} %v_ref.1, bf16[2,64,3,8,128]{4,3,2,1,0:T(8,128)(2,1)} %bitcast.6, bf16[2,64,3,8,128]{4,3,2,1,0:T(8,128)(2,1)} %bitcast.7), custom_call_target="tpu_custom_call" | custom-call | tf_op jit(solution)/shard_map/caches/pallas_call | solution.py:526
  422.0 0.0 copy-done
  422.0 1.1 copy.23
  (4 shorter events, 0.0 us)
Async XLA Ops:
  1.4 0.6 copy-start.1
  394.1 27.9 %copy-start = (bf16[3,128,2048]{2,1,0:T(8,128)(2,1)S(1)}, bf16[3,128,2048]{2,1,0:T(8,128)(2,1)}, u32[]{:S(2)}) copy-start(bf16[3,128,2048]{2,1,0:T(8,128)(2,1)} %get-tuple-element.21) | copy-start | bytes 4718596

commit v2 on v1

--- a/solution.py
+++ b/solution.py
@@ -82,13 +82,13 @@
     def qkv_load(l, n):
         j, c0 = QKV_TILES[n]
         src = (wq_ref, wk_ref, wv_ref)[n // 2]
-        return lc(src.at[l, :, pl.ds((n % 2) * TW, TW)], W1.at[j, :, pl.ds(c0, TW)], q_wsem.at[n])
+        return lc(src.at[l, :, pl.ds((n % 2) * TW, TW)], W1.at[j, pl.ds(0, DW), pl.ds(c0, TW)], q_wsem.at[n])
 
     def qkv_loads(l):
         return [qkv_load(l, n) for n in range(6)]
 
     def gu_loads(l):
-        return [lc((wg_ref, wu_ref)[j].at[l, pl.ds(r * 512, 512)], W1.at[j, pl.ds(r * 512, 512)], g_wsem.at[j * 4 + r]) for r in range(4) for j in range(2)]
+        return [lc((wg_ref, wu_ref)[j].at[l, pl.ds(r * 688, 688)], W1.at[j, pl.ds(r * 688, 688)], g_wsem.at[j * 4 + r]) for r in range(4) for j in range(2)]
 
     def wo_loads(l):
         return [lc(wo_ref.at[l], WO, o_wsem.at[0])]
@@ -124,9 +124,12 @@
     def tile_copy(m, j, n, c0, w):
         return rc(GP.at[m, j, oy, :, pl.ds(c0, w)], GR.at[m, j, :, pl.ds(c0, w)], g_ss.at[m, j, n], g_rs.at[m, j, n], ypeer)
 
-    def compute_tile(m, j, c0, w):
+    def compute_tile(m, j, c0, w, transposed=False):
         xm = X[m].reshape(2 * R, DW)
-        res = dot(xm, W1[j, :, pl.ds(c0, w)]).astype(BF)
+        if transposed:
+            res = dot_t(xm, W1[j, pl.ds(c0, w), :]).astype(BF)
+        else:
+            res = dot(xm, W1[j, pl.ds(0, DW), pl.ds(c0, w)]).astype(BF)
         GP[m, j, :, :, pl.ds(c0, w)] = res.reshape(2, R, w)
 
     def phase_q(m, l, first):
@@ -148,13 +151,13 @@
         def body(i, _):
             c0 = pl.multiple_of(i * TW, TW)
             for j in range(2):
-                compute_tile(m, j, c0, TW)
+                compute_tile(m, j, c0, TW, True)
                 if send:
                     tile_copy(m, j, i, c0, TW).start()
             return 0
         lax.fori_loop(0, 5, body, 0)
         for j in range(2):
-            compute_tile(m, j, 2560, 192)
+            compute_tile(m, j, 2560, 192, True)
             if send:
                 tile_copy(m, j, 5, 2560, 256).start()
 
@@ -219,7 +222,7 @@
                 scale = RSC[j, rows]
                 for h in range(8):
                     z = GR[m, 0, rows, pl.ds((j * 8 + h) * 128, 128)].astype(F32)
-                    z = z * scale * gain[l, :, pl.ds(h * 128, 128)]
+                    z = z * scale * gain[pl.ds(l, 1), pl.ds(h * 128, 128)].astype(F32)
                     rot = z * cosv + pltpu.roll(z, 64, 1) * sinv
                     out[t, dst, h, :] = rot.astype(BF).astype(F32)
             for h in range(8):
@@ -358,7 +361,7 @@
             scale = RSC[y, rows]
             for h in range(16):
                 cols = pl.ds(h * 128, 128)
-                X[m, y, rows, cols] = (X[m, y, rows, cols].astype(F32) + AF[m, arow, cols].astype(F32) * scale * gain[l, :, cols]).astype(BF)
+                X[m, y, rows, cols] = (X[m, y, rows, cols].astype(F32) + AF[m, arow, cols].astype(F32) * scale * gain[pl.ds(l, 1), cols].astype(F32)).astype(BF)
             return 0
         lax.fori_loop(0, 2 * R // 16, body, 0)
 
@@ -473,7 +476,6 @@
         cos_part, sin_part = jnp.cos(ang), jnp.sin(ang)
         cos2 = jnp.concatenate([cos_part, cos_part], axis=-1)
         sin2 = jnp.concatenate([-sin_part, sin_part], axis=-1)
-        gains = [g.astype(F32).reshape(L, 1, -1) for g in (q_gain, k_gain, attn_gain, mlp_gain)]
         hbm = pl.BlockSpec(memory_space=pl.ANY)
         vm = pl.BlockSpec(memory_space=pltpu.VMEM)
         dma = pltpu.SemaphoreType.DMA
@@ -488,7 +490,7 @@
             out_specs=[hbm] * 3,
             scratch_shapes=[
                 pltpu.VMEM((NB, 2, R, DW), BF),
-                pltpu.VMEM((2, DW, FW), BF),
+                pltpu.VMEM((2, FW, DW), BF),
                 pltpu.VMEM((QW, DW), BF),
                 pltpu.VMEM((FW, DW), BF),
                 pltpu.VMEM((NB, 2, 2, R, FP), BF),
@@ -519,7 +521,7 @@
             compiler_params=pltpu.CompilerParams(collective_id=0, has_side_effects=True, vmem_limit_bytes=67043328),
             name="layers",
         )(start_local, embeds, k_cache.reshape(L, rows, SH, HEAD_DIM), v_cache.reshape(L, rows, SH, HEAD_DIM),
-          w_query, w_key, w_value, w_out, w_gate, w_up, w_down, *gains, cos2, sin2)
+          w_query, w_key, w_value, w_out, w_gate.transpose(0, 2, 1), w_up.transpose(0, 2, 1), w_down, q_gain, k_gain, attn_gain, mlp_gain, cos2, sin2)
         bc = 8
         big = pl.BlockSpec((1, bc, SEQ, HL, HEAD_DIM), lambda l, c, s: (l, c, 0, 0, 0))
         small = pl.BlockSpec((1, bc, T, HL, HEAD_DIM), lambda l, c, s: (l, c, 0, 0, 0))

time: 425 us -> 366 us (0.86)
  local copies, waits for them, and re-layouts: 66.4 us -> 2.7 us
  Pallas kernels: 355 us -> 361 us
    unnamed x7 -> x5, local copies, waits for them, and re-layouts: 60.2 us -> 1.72 us
    pallas_call x1, Pallas kernels: 327 us -> 333 us  [device_fn(): pl.pallas_call(main_kernel, out_shape=[jax.ShapeDtypeStruct(embeds.shape,...]
    reshape x4 -> x0, local copies, waits for them, and re-layouts: 5.19 us -> none  [device_fn(): g.astype(F32).reshape(L, 1, -1)]
where the time goes in v2:
time: 366 us; the launch traced here: 365 us
  Pallas kernels  361 us (99%)
    pallas_call x1, Pallas kernels, device_fn(): pl.pallas_call(main_kernel, out_shape=[jax.ShapeDtypeStruct(embeds.shape,...  333 us
    pallas_call x1, Pallas kernels, device_fn(): pl.pallas_call(cache_kernel, out_shape=[jax.ShapeDtypeStruct(k_cache.shap...  27.9 us

profile of v2, /device:TPU:0, one launch (start us, length us, event | category | flops | bytes accessed | tf_op | source)
XLA Modules:
  0.0 365.2 jit_solution(6690159824760902894)
XLA Ops:
  0.6 0.7 dynamic_slice.3.start_ref
  1.4 0.0 copy-start.1
  1.4 0.6 copy-done.1
  1.9 0.1 add.30
  2.0 0.1 add.34
  2.1 0.1 add.32
  2.2 0.4 fusion
  2.6 0.8 pad_maximum_fusion
  3.4 332.7 %layers.1 = (bf16[3,128,2048]{2,1,0:T(8,128)(2,1)}, bf16[2,64,24,128]{3,2,1,0:T(8,128)(2,1)}, bf16[2,64,24,128]{3,2,1,0:T(8,128)(2,1)}) custom-call(s32[64]{0:T(128)} %copy-done.1, bf16[3,128,2048]{2,1,0:T(8,128)(2,1)} %emb_ref.1, bf16[2,64,512,128]{3,2,1,0:T(8,128)(2,1)} %bitcast.6, bf16[2,64,512,128]{3,2,1,0:T(8,128)(2,1)} %bitcast.7, ...), custom_call_target="tpu_custom_call" | custom-call | tf_op jit(solution)/shard_map/layers/pallas_call | solution.py:482
  336.2 0.0 copy-start
  336.2 27.9 %caches.1 = (bf16[2,64,64,8,128]{4,3,2,1,0:T(8,128)(2,1)}, bf16[2,64,64,8,128]{4,3,2,1,0:T(8,128)(2,1)}) custom-call(s32[64]{0:T(128)} %copy-done.1, bf16[2,64,64,8,128]{4,3,2,1,0:T(8,128)(2,1)} %k_ref.1, bf16[2,64,64,8,128]{4,3,2,1,0:T(8,128)(2,1)} %v_ref.1, bf16[2,64,3,8,128]{4,3,2,1,0:T(8,128)(2,1)} %bitcast.10, bf16[2,64,3,8,128]{4,3,2,1,0:T(8,128)(2,1)} %bitcast.11), custom_call_target="tpu_custom_call" | custom-call | tf_op jit(solution)/shard_map/caches/pallas_call | solution.py:528
  364.1 0.0 copy-done
  364.1 1.1 copy.19
  (4 shorter events, 0.0 us)
Async XLA Ops:
  1.4 0.6 copy-start.1
  336.2 27.9 %copy-start = (bf16[3,128,2048]{2,1,0:T(8,128)(2,1)S(1)}, bf16[3,128,2048]{2,1,0:T(8,128)(2,1)}, u32[]{:S(2)}) copy-start(bf16[3,128,2048]{2,1,0:T(8,128)(2,1)} %get-tuple-element.21) | copy-start | bytes 4718596

commit v3 on v2

--- a/solution.py
+++ b/solution.py
@@ -30,6 +30,7 @@
 SH = SEQ * HL
 CB = 4
 NCH = RB // CB
+SLOTS = 4
 TW = 512
 HALF = DW // 2
 GU_TILES = [(0, 512), (512, 512), (1024, 512), (1536, 512), (2048, 512), (2560, 256)]
@@ -116,8 +117,8 @@
         pl.semaphore_signal(barrier, inc=1, device_id=dev, device_id_type=MESH)
     pl.semaphore_wait(barrier, 5)
 
-    start(kv_copies(0, 0, 0, 0))
-    start(kv_copies(0, 0, 1, 1))
+    for c in range(SLOTS):
+        start(kv_copies(0, 0, c, c))
     start(wo_loads(0))
     start(wd_loads(0))
 
@@ -147,22 +148,23 @@
                     return 0
                 lax.fori_loop(0, cnt, body, 0)
 
-    def phase_g(m, l, send):
+    def phase_g(m, sent):
         def body(i, _):
             c0 = pl.multiple_of(i * TW, TW)
             for j in range(2):
                 compute_tile(m, j, c0, TW, True)
-                if send:
+
+                @pl.when(i < sent)
+                def _():
                     tile_copy(m, j, i, c0, TW).start()
             return 0
         lax.fori_loop(0, 5, body, 0)
         for j in range(2):
             compute_tile(m, j, 2560, 192, True)
-            if send:
-                tile_copy(m, j, 5, 2560, 256).start()
-
-    def send_g(m):
-        for n, (c0, w) in enumerate(GU_TILES):
+
+    def send_g(m, lo, hi):
+        for n in range(lo, hi):
+            c0, w = GU_TILES[n]
             for j in range(2):
                 tile_copy(m, j, n, c0, w).start()
 
@@ -248,7 +250,7 @@
         newm = (lax.rem(rown, HL) == lax.rem(coln, HL)) & (coln <= rown)
 
         def chunk(c, _):
-            slot = lax.rem(c, 2)
+            slot = lax.rem(c, SLOTS)
             wait(kv_copies(l, m, c, slot))
             for k in range(CB):
                 i = c * CB + k
@@ -267,16 +269,16 @@
                 KO[m, i] = kn
                 VO[m, i] = vn
 
-            @pl.when(c < NCH - 2)
+            @pl.when(c < NCH - SLOTS)
             def _():
-                start(kv_copies(l, m, c + 2, slot))
+                start(kv_copies(l, m, c + SLOTS, slot))
             return 0
         lax.fori_loop(0, NCH, chunk, 0)
         start(ko_copies(l, m))
         nxt = (l, m + 1) if m + 1 < NB else (l + 1, 0)
         if nxt[0] < L:
-            start(kv_copies(nxt[0], nxt[1], 0, 0))
-            start(kv_copies(nxt[0], nxt[1], 1, 1))
+            for c in range(SLOTS):
+                start(kv_copies(nxt[0], nxt[1], c, c))
 
         def body(i, _):
             rows = pl.ds(pl.multiple_of(i * 16, 16), 16)
@@ -396,10 +398,10 @@
     phase_q(A, 0, True)
     phase_q(B, 0, False)
     for l in range(L):
-        start(gu_loads(l))
         phase_s(A)
         phase_t1(A, l)
         phase_t2(A, l)
+        start(gu_loads(l))
         phase_s(B)
         phase_t1(B, l)
         wait(wo_loads(l))
@@ -413,21 +415,23 @@
         if l + 1 < L:
             start(wo_loads(l + 1))
         wait(gu_loads(l))
-        phase_g(A, l, True)
+        phase_g(A, 3)
         phase_3(0, B)
+        send_g(A, 3, 6)
         phase_h(0, B, l)
-        phase_g(B, l, False)
+        phase_g(B, 0)
         if l + 1 < L:
             start(qkv_loads(l + 1))
         phase_c(A, 0, 6)
-        send_g(B)
+        send_g(B, 0, 3)
         wait(wd_loads(l))
         phase_d(A, l)
         phase_2(1, A)
-        phase_c(B, 0, 3)
+        phase_c(B, 0, 2)
         phase_3(1, A)
+        send_g(B, 3, 6)
         phase_h(1, A, l)
-        phase_c(B, 3, 6)
+        phase_c(B, 2, 6)
         if l + 1 < L:
             phase_q(A, l + 1, True)
         else:
@@ -503,8 +507,8 @@
                 pltpu.VMEM((T, RB, HL, HEAD_DIM), F32),
                 pltpu.VMEM((NB, RB, T * HL, HEAD_DIM), BF),
                 pltpu.VMEM((NB, RB, T * HL, HEAD_DIM), BF),
-                pltpu.VMEM((2, CB, SH, HEAD_DIM), BF),
-                pltpu.VMEM((2, CB, SH, HEAD_DIM), BF),
+                pltpu.VMEM((SLOTS, CB, SH, HEAD_DIM), BF),
+                pltpu.VMEM((SLOTS, CB, SH, HEAD_DIM), BF),
                 pltpu.VMEM((NB, 2 * R, DW), BF),
                 pltpu.VMEM((NB, 2 * R, HALF), BF),
                 pltpu.VMEM((NB, 2 * R, HALF), BF),
@@ -514,7 +518,7 @@
                 pltpu.VMEM((2, R, 128), F32),
                 pltpu.VMEM((3, NB, 8, 128), F32),
                 pltpu.VMEM((3, NB, 3, 8, 128), F32),
-                dma((NB * 2 * T,)), dma((6,)), dma((8,)), dma((1,)), dma((4,)), dma((2, 2)), dma((2, NB)), dma((NB * 2 * T,)),
+                dma((NB * 2 * T,)), dma((6,)), dma((8,)), dma((1,)), dma((4,)), dma((2, SLOTS)), dma((2, NB)), dma((NB * 2 * T,)),
                 dma((NB, 2, 6)), dma((NB, 2, 6)), dma((NB, 6)), dma((NB, 6)), dma((NB,)), dma((NB,)),
                 dma((NB,)), dma((NB,)), dma((NB,)), dma((2, NB)), dma((NB,)), dma((NB,)), dma((3, NB, 3)), dma((3, NB, 3)),
             ],

time: 366 us -> 340 us (0.929)
  Pallas kernels: 361 us -> 336 us
    pallas_call x1, Pallas kernels: 333 us -> 308 us  [device_fn(): pl.pallas_call(main_kernel, out_shape=[jax.ShapeDtypeStruct(embeds.shape,...]
where the time goes in v3:
time: 340 us
  Pallas kernels  336 us (99%)
    pallas_call x1, Pallas kernels, device_fn(): pl.pallas_call(main_kernel, out_shape=[jax.ShapeDtypeStruct(embeds.shape,...  308 us
    pallas_call x1, Pallas kernels, device_fn(): pl.pallas_call(cache_kernel, out_shape=[jax.ShapeDtypeStruct(k_cache.shap...  27.9 us

profile of v3, /device:TPU:0, one launch (start us, length us, event | category | flops | bytes accessed | tf_op | source)
XLA Modules:
  0.0 340.1 jit_solution(2783371290652919617)
XLA Ops:
  0.6 0.7 dynamic_slice.3.start_ref
  1.4 0.0 copy-start.1
  1.4 0.6 copy-done.1
  1.9 0.1 add.30
  2.0 0.1 add.34
  2.1 0.1 add.32
  2.2 0.4 fusion
  2.6 0.8 pad_maximum_fusion
  3.4 307.6 %layers.1 = (bf16[3,128,2048]{2,1,0:T(8,128)(2,1)}, bf16[2,64,24,128]{3,2,1,0:T(8,128)(2,1)}, bf16[2,64,24,128]{3,2,1,0:T(8,128)(2,1)}) custom-call(s32[64]{0:T(128)} %copy-done.1, bf16[3,128,2048]{2,1,0:T(8,128)(2,1)} %emb_ref.1, bf16[2,64,512,128]{3,2,1,0:T(8,128)(2,1)} %bitcast.6, bf16[2,64,512,128]{3,2,1,0:T(8,128)(2,1)} %bitcast.7, ...), custom_call_target="tpu_custom_call" | custom-call | tf_op jit(solution)/shard_map/layers/pallas_call | solution.py:486
  311.1 0.0 copy-start
  311.1 27.9 %caches.1 = (bf16[2,64,64,8,128]{4,3,2,1,0:T(8,128)(2,1)}, bf16[2,64,64,8,128]{4,3,2,1,0:T(8,128)(2,1)}) custom-call(s32[64]{0:T(128)} %copy-done.1, bf16[2,64,64,8,128]{4,3,2,1,0:T(8,128)(2,1)} %k_ref.1, bf16[2,64,64,8,128]{4,3,2,1,0:T(8,128)(2,1)} %v_ref.1, bf16[2,64,3,8,128]{4,3,2,1,0:T(8,128)(2,1)} %bitcast.10, bf16[2,64,3,8,128]{4,3,2,1,0:T(8,128)(2,1)} %bitcast.11), custom_call_target="tpu_custom_call" | custom-call | tf_op jit(solution)/shard_map/caches/pallas_call | solution.py:532
  339.0 0.0 copy-done
  339.0 1.1 copy.19
  (4 shorter events, 0.0 us)
Async XLA Ops:
  1.4 0.6 copy-start.1
  311.1 27.9 %copy-start = (bf16[3,128,2048]{2,1,0:T(8,128)(2,1)S(1)}, bf16[3,128,2048]{2,1,0:T(8,128)(2,1)}, u32[]{:S(2)}) copy-start(bf16[3,128,2048]{2,1,0:T(8,128)(2,1)} %get-tuple-element.21) | copy-start | bytes 4718596

commit v4 on v3

--- a/solution.py
+++ b/solution.py
@@ -18,8 +18,8 @@
 
 L = 2
 T = 3
-NB = 2
-RB = 32
+NB = 4
+RB = 16
 R = T * RB
 HL = 8
 DW = 2048
@@ -33,8 +33,216 @@
 SLOTS = 4
 TW = 512
 HALF = DW // 2
+RC = R // 16
 GU_TILES = [(0, 512), (512, 512), (1024, 512), (1536, 512), (2048, 512), (2560, 256)]
 QKV_TILES = [(0, 0), (0, 512), (0, 1024), (0, 1536), (1, 0), (1, 512)]
+
+
+ORDER = [
+    ("Q", 0, 0),
+    ("Qs", 0, 0, 0, 6),
+    ("Q", 1, 0),
+    ("Qs", 1, 0, 0, 4),
+    ("Q", 2, 0),
+    ("Qs", 1, 0, 4, 6),
+    ("Q", 3, 0),
+    ("S", 0, 0),
+    ("T", 0, 0),
+    ("Qs", 2, 0, 0, 2),
+    ("Lg", 0),
+    ("Qs", 2, 0, 2, 4),
+    ("O", 0, 0),
+    ("S", 1, 0),
+    ("2", 0, 0, 0),
+    ("Qs", 2, 0, 4, 6),
+    ("Qs", 3, 0, 0, 2),
+    ("T", 1, 0),
+    ("S", 2, 0),
+    ("3", 0, 0, 0),
+    ("Qs", 3, 0, 2, 6),
+    ("T", 2, 0),
+    ("H", 0, 0, 0),
+    ("G", 0, 0),
+    ("Gs", 0, 0, 0, 4),
+    ("S", 3, 0),
+    ("O", 1, 0),
+    ("2", 0, 1, 0),
+    ("C", 0, 0, 0, 1),
+    ("3", 0, 1, 0),
+    ("Gs", 0, 0, 4, 5),
+    ("C", 0, 0, 1, 3),
+    ("O", 2, 0),
+    ("C", 0, 0, 3, 4),
+    ("T", 3, 0),
+    ("2", 0, 2, 0),
+    ("H", 0, 1, 0),
+    ("Gs", 0, 0, 5, 6),
+    ("G", 1, 0),
+    ("Gs", 1, 0, 0, 2),
+    ("C", 0, 0, 4, 5),
+    ("O", 3, 0),
+    ("3", 0, 2, 0),
+    ("2", 0, 3, 0),
+    ("Gs", 1, 0, 2, 4),
+    ("H", 0, 2, 0),
+    ("C", 0, 0, 5, 6),
+    ("C", 1, 0, 0, 3),
+    ("3", 0, 3, 0),
+    ("Gs", 1, 0, 4, 5),
+    ("G", 2, 0),
+    ("Gs", 2, 0, 0, 1),
+    ("D", 0, 0),
+    ("Gs", 2, 0, 1, 2),
+    ("H", 0, 3, 0),
+    ("Gs", 1, 0, 5, 6),
+    ("C", 1, 0, 3, 4),
+    ("2", 1, 0, 0),
+    ("Gs", 2, 0, 2, 3),
+    ("C", 2, 0, 0, 1),
+    ("C", 1, 0, 4, 5),
+    ("G", 3, 0),
+    ("Gs", 3, 0, 0, 1),
+    ("Lo", 1),
+    ("3", 1, 0, 0),
+    ("Gs", 3, 0, 1, 2),
+    ("C", 3, 0, 0, 1),
+    ("C", 1, 0, 5, 6),
+    ("C", 2, 0, 1, 2),
+    ("Gs", 2, 0, 3, 4),
+    ("C", 2, 0, 2, 3),
+    ("D", 1, 0),
+    ("Gs", 3, 0, 2, 4),
+    ("H", 1, 0, 0),
+    ("2", 1, 1, 0),
+    ("Gs", 2, 0, 4, 5),
+    ("C", 3, 0, 1, 2),
+    ("3", 1, 1, 0),
+    ("Lq", 1),
+    ("Gs", 2, 0, 5, 6),
+    ("C", 3, 0, 2, 3),
+    ("Gs", 3, 0, 4, 5),
+    ("C", 3, 0, 3, 4),
+    ("C", 2, 0, 3, 4),
+    ("Q", 0, 1),
+    ("Gs", 3, 0, 5, 6),
+    ("C", 2, 0, 4, 5),
+    ("H", 1, 1, 0),
+    ("C", 2, 0, 5, 6),
+    ("Qs", 0, 1, 0, 4),
+    ("C", 3, 0, 4, 6),
+    ("Qs", 0, 1, 4, 6),
+    ("D", 2, 0),
+    ("Q", 1, 1),
+    ("Qs", 1, 1, 0, 2),
+    ("2", 1, 2, 0),
+    ("Qs", 1, 1, 2, 4),
+    ("D", 3, 0),
+    ("S", 0, 1),
+    ("3", 1, 2, 0),
+    ("2", 1, 3, 0),
+    ("Qs", 1, 1, 4, 6),
+    ("T", 0, 1),
+    ("H", 1, 2, 0),
+    ("Q", 2, 1),
+    ("Qs", 2, 1, 0, 2),
+    ("S", 1, 1),
+    ("3", 1, 3, 0),
+    ("O", 0, 1),
+    ("Qs", 2, 1, 2, 6),
+    ("T", 1, 1),
+    ("2", 0, 0, 1),
+    ("H", 1, 3, 0),
+    ("Q", 3, 1),
+    ("Lg", 1),
+    ("S", 2, 1),
+    ("Qs", 3, 1, 0, 2),
+    ("3", 0, 0, 1),
+    ("Qs", 3, 1, 2, 4),
+    ("O", 1, 1),
+    ("T", 2, 1),
+    ("2", 0, 1, 1),
+    ("H", 0, 0, 1),
+    ("Qs", 3, 1, 4, 6),
+    ("G", 0, 1),
+    ("Gs", 0, 1, 0, 1),
+    ("3", 0, 1, 1),
+    ("Gs", 0, 1, 1, 3),
+    ("S", 3, 1),
+    ("O", 2, 1),
+    ("C", 0, 1, 0, 1),
+    ("2", 0, 2, 1),
+    ("T", 3, 1),
+    ("Gs", 0, 1, 3, 5),
+    ("H", 0, 1, 1),
+    ("G", 1, 1),
+    ("O", 3, 1),
+    ("Gs", 1, 1, 0, 1),
+    ("3", 0, 2, 1),
+    ("Gs", 1, 1, 1, 3),
+    ("H", 0, 2, 1),
+    ("2", 0, 3, 1),
+    ("C", 0, 1, 1, 2),
+    ("C", 1, 1, 0, 1),
+    ("Gs", 1, 1, 3, 4),
+    ("G", 2, 1),
+    ("Gs", 1, 1, 4, 5),
+    ("Gs", 2, 1, 0, 1),
+    ("Gs", 0, 1, 5, 6),
+    ("Gs", 2, 1, 1, 2),
+    ("C", 1, 1, 1, 2),
+    ("3", 0, 3, 1),
+    ("C", 1, 1, 2, 3),
+    ("C", 2, 1, 0, 1),
+    ("C", 1, 1, 3, 4),
+    ("H", 0, 3, 1),
+    ("C", 2, 1, 1, 2),
+    ("Gs", 2, 1, 2, 3),
+    ("Gs", 1, 1, 5, 6),
+    ("C", 0, 1, 2, 4),
+    ("Gs", 2, 1, 3, 4),
+    ("C", 2, 1, 2, 3),
+    ("Gs", 2, 1, 4, 5),
+    ("C", 1, 1, 4, 5),
+    ("Gs", 2, 1, 5, 6),
+    ("C", 2, 1, 3, 4),
+    ("C", 0, 1, 4, 5),
+    ("G", 3, 1),
+    ("C", 0, 1, 5, 6),
+    ("C", 2, 1, 4, 5),
+    ("Gs", 3, 1, 0, 1),
+    ("C", 1, 1, 5, 6),
+    ("Gs", 3, 1, 1, 2),
+    ("Ld", 1),
+    ("C", 3, 1, 0, 1),
+    ("Gs", 3, 1, 2, 3),
+    ("D", 0, 1),
+    ("C", 2, 1, 5, 6),
+    ("Gs", 3, 1, 3, 4),
+    ("D", 1, 1),
+    ("C", 3, 1, 1, 2),
+    ("Gs", 3, 1, 4, 6),
+    ("2", 1, 0, 1),
+    ("C", 3, 1, 2, 3),
+    ("2", 1, 1, 1),
+    ("C", 3, 1, 3, 5),
+    ("D", 2, 1),
+    ("C", 3, 1, 5, 6),
+    ("2", 1, 2, 1),
+    ("D", 3, 1),
+    ("2", 1, 3, 1),
+    ("3", 1, 0, 1),
+    ("3", 1, 2, 1),
+    ("H", 1, 0, 1),
+    ("3", 1, 1, 1),
+    ("3", 1, 3, 1),
+    ("H", 1, 1, 1),
+    ("H", 1, 2, 1),
+    ("H", 1, 3, 1),
+]
+
+
+def lane_fold(z):
+    return jnp.broadcast_to(jnp.sum(z, axis=1, keepdims=True), (z.shape[0], 128))
 
 
 def dot(a, b):
@@ -133,48 +341,48 @@
             res = dot(xm, W1[j, pl.ds(0, DW), pl.ds(c0, w)]).astype(BF)
         GP[m, j, :, :, pl.ds(c0, w)] = res.reshape(2, R, w)
 
-    def phase_q(m, l, first):
+    def phase_q(m, l, fresh):
         for j, cnt in ((0, 4), (1, 2)):
-            if first:
+            if fresh:
                 for i in range(cnt):
                     qkv_load(l, j * 4 + i).wait()
-                    compute_tile(m, j, i * TW, TW)
-                    tile_copy(m, j, i, i * TW, TW).start()
-            else:
-                def body(i, _):
-                    c0 = pl.multiple_of(i * TW, TW)
-                    compute_tile(m, j, c0, TW)
-                    tile_copy(m, j, i, c0, TW).start()
-                    return 0
-                lax.fori_loop(0, cnt, body, 0)
-
-    def phase_g(m, sent):
+
+            def body(i, _):
+                compute_tile(m, j, pl.multiple_of(i * TW, TW), TW)
+                return 0
+            lax.fori_loop(0, cnt, body, 0)
+
+    def send_q(m, lo, hi):
+        for j, c0 in QKV_TILES[lo:hi]:
+            tile_copy(m, j, c0 // TW, c0, TW).start()
+
+    def phase_g(m):
         def body(i, _):
-            c0 = pl.multiple_of(i * TW, TW)
             for j in range(2):
-                compute_tile(m, j, c0, TW, True)
-
-                @pl.when(i < sent)
-                def _():
-                    tile_copy(m, j, i, c0, TW).start()
+                compute_tile(m, j, pl.multiple_of(i * TW, TW), TW, True)
             return 0
         lax.fori_loop(0, 5, body, 0)
         for j in range(2):
             compute_tile(m, j, 2560, 192, True)
 
     def send_g(m, lo, hi):
-        for n in range(lo, hi):
-            c0, w = GU_TILES[n]
+        def body(n, _):
             for j in range(2):
-                tile_copy(m, j, n, c0, w).start()
+                tile_copy(m, j, n, pl.multiple_of(n * TW, TW), TW).start()
+            return 0
+        if lo < 5:
+            lax.fori_loop(lo, min(hi, 5), body, 0)
+        if hi == 6:
+            for j in range(2):
+                tile_copy(m, j, 5, 2560, 256).start()
 
     def stat_copies(kind, m):
         peers = (cpeer, xpeer, xdiag) if kind == 0 else (cpeer, ypeer, ydiag)
         return [rc(ST.at[kind, m], SR.at[kind, m, k], st_ss.at[kind, m, k], st_rs.at[kind, m, k], peers[k]) for k in range(3)]
 
     def stat_send(kind, m):
-        v0 = jnp.sum(RSUM[0], axis=1, keepdims=True)
-        v1 = jnp.sum(RSUM[1], axis=1, keepdims=True)
+        v0 = RSUM[0]
+        v1 = RSUM[1]
         lane = lax.broadcasted_iota(jnp.int32, (R, 128), 1)
         both = jnp.where(lane == 0, v0, v1)
         full = jnp.concatenate([both, jnp.zeros((128 - R, 128), F32)], axis=0)
@@ -195,18 +403,15 @@
 
         def body(i, _):
             rows = pl.ds(pl.multiple_of(i * 16, 16), 16)
-            for j in range(2):
-                acc = jnp.zeros((16, 128), F32)
-                for h in range(8):
-                    cols = pl.ds((j * 8 + h) * 128, 128)
-                    z = (GP[m, 0, ty, rows, cols].astype(F32) + GR[m, 0, rows, cols].astype(F32)).astype(BF)
-                    GR[m, 0, rows, cols] = z
-                    zf = z.astype(F32)
-                    acc = acc + zf * zf
-                RSUM[j, rows] = acc
-            for h in range(8):
-                cols = pl.ds(h * 128, 128)
-                GR[m, 1, rows, cols] = (GP[m, 1, ty, rows, cols].astype(F32) + GR[m, 1, rows, cols].astype(F32)).astype(BF)
+            qk = pl.ds(0, 2 * QW)
+            z = (GP[m, 0, ty, rows, qk].astype(F32) + GR[m, 0, rows, qk].astype(F32)).astype(BF)
+            GR[m, 0, rows, qk] = z
+            zf = z.astype(F32)
+            sq = zf * zf
+            RSUM[0, rows] = lane_fold(sq[:, :QW])
+            RSUM[1, rows] = lane_fold(sq[:, QW:])
+            cols = pl.ds(0, QW)
+            GR[m, 1, rows, cols] = (GP[m, 1, ty, rows, cols].astype(F32) + GR[m, 1, rows, cols].astype(F32)).astype(BF)
             return 0
         lax.fori_loop(0, R // 16, body, 0)
         stat_send(0, m)
@@ -214,21 +419,21 @@
     def phase_t1(m, l):
         stat_recv(0, m)
 
+        gain = jnp.concatenate([qg_ref[pl.ds(l, 1)], kg_ref[pl.ds(l, 1)]], axis=1).astype(F32)
+        low = lax.rem(lax.broadcasted_iota(jnp.int32, (16, 2 * QW), 1), HEAD_DIM) < HEAD_DIM // 2
+
         def body(i, _):
             rows = pl.ds(pl.multiple_of(i * 16, 16), 16)
-            t = i // 2
-            dst = pl.ds(pl.multiple_of(lax.rem(i, 2) * 16, 16), 16)
-            cosv = cos_ref[m, rows]
-            sinv = sin_ref[m, rows]
-            for j, (out, gain) in enumerate(((QS, qg_ref), (KS, kg_ref))):
-                scale = RSC[j, rows]
-                for h in range(8):
-                    z = GR[m, 0, rows, pl.ds((j * 8 + h) * 128, 128)].astype(F32)
-                    z = z * scale * gain[pl.ds(l, 1), pl.ds(h * 128, 128)].astype(F32)
-                    rot = z * cosv + pltpu.roll(z, 64, 1) * sinv
-                    out[t, dst, h, :] = rot.astype(BF).astype(F32)
-            for h in range(8):
-                VS[t, dst, h, :] = GR[m, 1, rows, pl.ds(h * 128, 128)].astype(F32)
+            scale = jnp.concatenate([RSC[0, rows]] * HL + [RSC[1, rows]] * HL, axis=1)
+            z = GR[m, 0, rows, pl.ds(0, 2 * QW)].astype(F32) * scale * gain
+            turned = jnp.where(low, pltpu.roll(z, 2 * QW - HEAD_DIM // 2, 1), pltpu.roll(z, HEAD_DIM // 2, 1))
+            rot = z * jnp.concatenate([cos_ref[m, rows]] * (2 * HL), axis=1) + turned * jnp.concatenate([sin_ref[m, rows]] * (2 * HL), axis=1)
+            rot = rot.astype(BF).astype(F32)
+            v = GR[m, 1, rows, pl.ds(0, QW)].astype(F32)
+            for h in range(HL):
+                QS[i, :, h, :] = rot[:, h * HEAD_DIM:(h + 1) * HEAD_DIM]
+                KS[i, :, h, :] = rot[:, QW + h * HEAD_DIM:QW + (h + 1) * HEAD_DIM]
+                VS[i, :, h, :] = v[:, h * HEAD_DIM:(h + 1) * HEAD_DIM]
             return 0
         lax.fori_loop(0, R // 16, body, 0)
 
@@ -249,8 +454,10 @@
         coln = lax.broadcasted_iota(jnp.int32, (T * HL, T * HL), 1)
         newm = (lax.rem(rown, HL) == lax.rem(coln, HL)) & (coln <= rown)
 
+        nxt = (l, m + 1) if m + 1 < NB else (l + 1, 0)
+
         def chunk(c, _):
-            slot = lax.rem(c, SLOTS)
+            slot = c
             wait(kv_copies(l, m, c, slot))
             for k in range(CB):
                 i = c * CB + k
@@ -268,24 +475,16 @@
                 OS[:, i] = o.reshape(T, HL, HEAD_DIM)
                 KO[m, i] = kn
                 VO[m, i] = vn
-
-            @pl.when(c < NCH - SLOTS)
-            def _():
-                start(kv_copies(l, m, c + SLOTS, slot))
+            if nxt[0] < L:
+                start(kv_copies(nxt[0], nxt[1], c, slot))
             return 0
         lax.fori_loop(0, NCH, chunk, 0)
         start(ko_copies(l, m))
-        nxt = (l, m + 1) if m + 1 < NB else (l + 1, 0)
-        if nxt[0] < L:
-            for c in range(SLOTS):
-                start(kv_copies(nxt[0], nxt[1], c, c))
 
         def body(i, _):
             rows = pl.ds(pl.multiple_of(i * 16, 16), 16)
-            t = i // 2
-            src = pl.ds(pl.multiple_of(lax.rem(i, 2) * 16, 16), 16)
             for h in range(8):
-                OB[m, ty, rows, pl.ds(h * 128, 128)] = OS[t, src, h, :].astype(BF)
+                OB[m, ty, rows, pl.ds(h * 128, 128)] = OS[i, :, h, :].astype(BF)
             return 0
         lax.fori_loop(0, R // 16, body, 0)
         o_copy(m).start()
@@ -341,11 +540,8 @@
             z = (XS[m, rows].astype(F32) + XR[ph, m, rows].astype(F32)).astype(BF)
             AF[m, rows, own_half] = z
             zf = z.astype(F32)
-            sq = zf * zf
-            acc = sq[:, 0:128]
-            for h in range(1, 8):
-                acc = acc + sq[:, h * 128:(h + 1) * 128]
-            RSUM[i // 6, pl.ds(pl.multiple_of(lax.rem(i, 6) * 16, 16), 16)] = acc
+            acc = lane_fold(zf * zf)
+            RSUM[i // RC, pl.ds(pl.multiple_of(lax.rem(i, RC) * 16, 16), 16)] = acc
             return 0
         lax.fori_loop(0, 2 * R // 16, body, 0)
         a_copy(m).start()
@@ -357,34 +553,39 @@
         a_copy(m).wait()
 
         def body(i, _):
-            y = i // 6
-            rows = pl.ds(pl.multiple_of(lax.rem(i, 6) * 16, 16), 16)
+            y = i // RC
+            rows = pl.ds(pl.multiple_of(lax.rem(i, RC) * 16, 16), 16)
             arow = pl.ds(pl.multiple_of(i * 16, 16), 16)
-            scale = RSC[y, rows]
-            for h in range(16):
-                cols = pl.ds(h * 128, 128)
-                X[m, y, rows, cols] = (X[m, y, rows, cols].astype(F32) + AF[m, arow, cols].astype(F32) * scale * gain[pl.ds(l, 1), cols].astype(F32)).astype(BF)
+            scale = jnp.concatenate([RSC[y, rows]] * 16, axis=1)
+            X[m, y, rows] = (X[m, y, rows].astype(F32) + AF[m, arow].astype(F32) * scale * gain[pl.ds(l, 1)].astype(F32)).astype(BF)
             return 0
         lax.fori_loop(0, 2 * R // 16, body, 0)
 
     def c_copy(m, n, c0, w):
         return rc(C.at[m, ty, :, pl.ds(c0, w)], C.at[m, ty, :, pl.ds(c0, w)], c_ss.at[m, n], c_rs.at[m, n], ypeer)
 
+    def c_tile(m, n, c0, w):
+        for j in range(2):
+            tile_copy(m, j, n, c0, w).wait()
+
+        def body(i, _):
+            rows = pl.ds(pl.multiple_of(i * 16, 16), 16)
+            cols = pl.ds(c0, w)
+            g = (GP[m, 0, ty, rows, cols].astype(F32) + GR[m, 0, rows, cols].astype(F32)).astype(BF).astype(F32)
+            u = (GP[m, 1, ty, rows, cols].astype(F32) + GR[m, 1, rows, cols].astype(F32)).astype(BF).astype(F32)
+            C[m, ty, rows, cols] = (jax.nn.silu(g) * u).astype(BF)
+            return 0
+        lax.fori_loop(0, R // 16, body, 0)
+        c_copy(m, n, c0, w).start()
+
     def phase_c(m, lo, hi):
-        for n in range(lo, hi):
-            c0, w = GU_TILES[n]
-            for j in range(2):
-                tile_copy(m, j, n, c0, w).wait()
-
-            def body(i, _):
-                rows = pl.ds(pl.multiple_of(i * 16, 16), 16)
-                cols = pl.ds(c0, w)
-                g = (GP[m, 0, ty, rows, cols].astype(F32) + GR[m, 0, rows, cols].astype(F32)).astype(BF).astype(F32)
-                u = (GP[m, 1, ty, rows, cols].astype(F32) + GR[m, 1, rows, cols].astype(F32)).astype(BF).astype(F32)
-                C[m, ty, rows, cols] = (jax.nn.silu(g) * u).astype(BF)
-                return 0
-            lax.fori_loop(0, R // 16, body, 0)
-            c_copy(m, n, c0, w).start()
+        def body(n, _):
+            c_tile(m, n, pl.multiple_of(n * TW, TW), TW)
+            return 0
+        if lo < 5:
+            lax.fori_loop(lo, min(hi, 5), body, 0)
+        if hi == 6:
+            c_tile(m, 5, 2560, 256)
 
     def y_copies(m):
         out = []
@@ -393,61 +594,65 @@
                 out.append(lc(X.at[m, y, pl.ds(t * RB, RB)], y_ref.at[t, pl.ds(y * NB * RB + m * RB, RB)], y_sem.at[(m * 2 + y) * T + t]))
         return out
 
-    A, B = 0, 1
     wait(emb_copies())
-    phase_q(A, 0, True)
-    phase_q(B, 0, False)
-    for l in range(L):
-        phase_s(A)
-        phase_t1(A, l)
-        phase_t2(A, l)
-        start(gu_loads(l))
-        phase_s(B)
-        phase_t1(B, l)
-        wait(wo_loads(l))
-        phase_o(A, l)
-        phase_2(0, A)
-        phase_t2(B, l)
-        phase_3(0, A)
-        phase_o(B, l)
-        phase_h(0, A, l)
-        phase_2(0, B)
-        if l + 1 < L:
-            start(wo_loads(l + 1))
-        wait(gu_loads(l))
-        phase_g(A, 3)
-        phase_3(0, B)
-        send_g(A, 3, 6)
-        phase_h(0, B, l)
-        phase_g(B, 0)
-        if l + 1 < L:
-            start(qkv_loads(l + 1))
-        phase_c(A, 0, 6)
-        send_g(B, 0, 3)
-        wait(wd_loads(l))
-        phase_d(A, l)
-        phase_2(1, A)
-        phase_c(B, 0, 2)
-        phase_3(1, A)
-        send_g(B, 3, 6)
-        phase_h(1, A, l)
-        phase_c(B, 2, 6)
-        if l + 1 < L:
-            phase_q(A, l + 1, True)
-        else:
-            start(y_copies(A))
-        phase_d(B, l)
-        if l + 1 < L:
-            start(wd_loads(l + 1))
-        phase_2(1, B)
-        phase_3(1, B)
-        phase_h(1, B, l)
-        if l + 1 < L:
-            phase_q(B, l + 1, False)
-        else:
-            start(y_copies(B))
-    wait(y_copies(A))
-    wait(y_copies(B))
+    seen = set()
+    for op, *arg in ORDER:
+        if op == "Lg":
+            start(gu_loads(arg[0]))
+        elif op == "Lq":
+            start(qkv_loads(arg[0]))
+        elif op == "Lo":
+            start(wo_loads(arg[0]))
+        elif op == "Ld":
+            start(wd_loads(arg[0]))
+        elif op == "Q":
+            m, l = arg
+            phase_q(m, l, ("q", l) not in seen)
+            seen.add(("q", l))
+        elif op == "Qs":
+            m, l, lo, hi = arg
+            send_q(m, lo, hi)
+        elif op == "S":
+            phase_s(arg[0])
+        elif op == "T":
+            m, l = arg
+            phase_t1(m, l)
+            phase_t2(m, l)
+        elif op == "O":
+            m, l = arg
+            if ("o", l) not in seen:
+                wait(wo_loads(l))
+                seen.add(("o", l))
+            phase_o(m, l)
+        elif op == "2":
+            phase_2(arg[0], arg[1])
+        elif op == "3":
+            phase_3(arg[0], arg[1])
+        elif op == "H":
+            ph, m, l = arg
+            phase_h(ph, m, l)
+            if ph == 1 and l == L - 1:
+                start(y_copies(m))
+        elif op == "G":
+            m, l = arg
+            if ("g", l) not in seen:
+                wait(gu_loads(l))
+                seen.add(("g", l))
+            phase_g(m)
+        elif op == "Gs":
+            m, l, lo, hi = arg
+            send_g(m, lo, hi)
+        elif op == "C":
+            m, l, lo, hi = arg
+            phase_c(m, lo, hi)
+        elif op == "D":
+            m, l = arg
+            if ("d", l) not in seen:
+                wait(wd_loads(l))
+                seen.add(("d", l))
+            phase_d(m, l)
+    for m in range(NB):
+        wait(y_copies(m))
     for m in range(NB):
         wait(ko_copies(L - 1, m))
 

time: 340 us -> 343 us (level)
  no operation moved by 1% of the time
where the time goes in v4:
time: 343 us; the launch traced here: 342 us
  Pallas kernels  338 us (99%)
    pallas_call x1, Pallas kernels, device_fn(): pl.pallas_call(main_kernel, out_shape=[jax.ShapeDtypeStruct(embeds.shape,...  310 us
    pallas_call x1, Pallas kernels, device_fn(): pl.pallas_call(cache_kernel, out_shape=[jax.ShapeDtypeStruct(k_cache.shap...  27.9 us

profile of v4, /device:TPU:0, one launch (start us, length us, event | category | flops | bytes accessed | tf_op | source)
XLA Modules:
  0.0 342.4 jit_solution(13763940191773080962)
XLA Ops:
  0.6 0.7 dynamic_slice.3.start_ref
  1.4 0.0 copy-start.1
  1.4 0.6 copy-done.1
  1.9 0.1 add.30
  2.0 0.1 add.34
  2.1 0.1 add.32
  2.2 0.4 fusion
  2.7 0.8 pad_maximum_fusion
  3.4 309.9 %layers.1 = (bf16[3,128,2048]{2,1,0:T(8,128)(2,1)}, bf16[2,64,24,128]{3,2,1,0:T(8,128)(2,1)}, bf16[2,64,24,128]{3,2,1,0:T(8,128)(2,1)}) custom-call(s32[64]{0:T(128)} %copy-done.1, bf16[3,128,2048]{2,1,0:T(8,128)(2,1)} %emb_ref.1, bf16[2,64,512,128]{3,2,1,0:T(8,128)(2,1)} %bitcast.6, bf16[2,64,512,128]{3,2,1,0:T(8,128)(2,1)} %bitcast.7, ...), custom_call_target="tpu_custom_call" | custom-call | tf_op jit(solution)/shard_map/layers/pallas_call | solution.py:691
  313.3 0.0 copy-start
  313.3 27.9 %caches.1 = (bf16[2,64,64,8,128]{4,3,2,1,0:T(8,128)(2,1)}, bf16[2,64,64,8,128]{4,3,2,1,0:T(8,128)(2,1)}) custom-call(s32[64]{0:T(128)} %copy-done.1, bf16[2,64,64,8,128]{4,3,2,1,0:T(8,128)(2,1)} %k_ref.1, bf16[2,64,64,8,128]{4,3,2,1,0:T(8,128)(2,1)} %v_ref.1, bf16[2,64,3,8,128]{4,3,2,1,0:T(8,128)(2,1)} %bitcast.10, bf16[2,64,3,8,128]{4,3,2,1,0:T(8,128)(2,1)} %bitcast.11), custom_call_target="tpu_custom_call" | custom-call | tf_op jit(solution)/shard_map/caches/pallas_call | solution.py:737
  341.2 0.0 copy-done
  341.2 1.1 copy.19
  (4 shorter events, 0.0 us)
Async XLA Ops:
  1.4 0.6 copy-start.1
  313.3 27.9 %copy-start = (bf16[3,128,2048]{2,1,0:T(8,128)(2,1)S(1)}, bf16[3,128,2048]{2,1,0:T(8,128)(2,1)}, u32[]{:S(2)}) copy-start(bf16[3,128,2048]{2,1,0:T(8,128)(2,1)} %get-tuple-element.21) | copy-start | bytes 4718596

commit v5 on v4

--- a/solution.py
+++ b/solution.py
@@ -34,209 +34,166 @@
 TW = 512
 HALF = DW // 2
 RC = R // 16
-GU_TILES = [(0, 512), (512, 512), (1024, 512), (1536, 512), (2048, 512), (2560, 256)]
+GU_SENDS = [(0, 1024), (1024, 1024), (2048, 768)]
 QKV_TILES = [(0, 0), (0, 512), (0, 1024), (0, 1536), (1, 0), (1, 512)]
 
 
 ORDER = [
     ("Q", 0, 0),
-    ("Qs", 0, 0, 0, 6),
+    ("Qs", 0, 0, 0, 1),
     ("Q", 1, 0),
-    ("Qs", 1, 0, 0, 4),
+    ("Qs", 0, 0, 1, 2),
+    ("Qs", 1, 0, 0, 1),
     ("Q", 2, 0),
-    ("Qs", 1, 0, 4, 6),
+    ("S", 0, 0),
+    ("Qs", 1, 0, 1, 2),
+    ("T", 0, 0),
     ("Q", 3, 0),
-    ("S", 0, 0),
-    ("T", 0, 0),
-    ("Qs", 2, 0, 0, 2),
+    ("Qs", 2, 0, 0, 1),
+    ("S", 1, 0),
+    ("Qs", 2, 0, 1, 2),
+    ("O", 0, 0),
+    ("2", 0, 0, 0),
     ("Lg", 0),
-    ("Qs", 2, 0, 2, 4),
-    ("O", 0, 0),
-    ("S", 1, 0),
-    ("2", 0, 0, 0),
-    ("Qs", 2, 0, 4, 6),
-    ("Qs", 3, 0, 0, 2),
     ("T", 1, 0),
+    ("Qs", 3, 0, 0, 1),
     ("S", 2, 0),
+    ("O", 1, 0),
     ("3", 0, 0, 0),
-    ("Qs", 3, 0, 2, 6),
     ("T", 2, 0),
+    ("Qs", 3, 0, 1, 2),
     ("H", 0, 0, 0),
     ("G", 0, 0),
-    ("Gs", 0, 0, 0, 4),
+    ("Gs", 0, 0, 0, 1),
+    ("O", 2, 0),
+    ("2", 0, 1, 0),
+    ("Gs", 0, 0, 1, 3),
     ("S", 3, 0),
-    ("O", 1, 0),
-    ("2", 0, 1, 0),
-    ("C", 0, 0, 0, 1),
     ("3", 0, 1, 0),
-    ("Gs", 0, 0, 4, 5),
-    ("C", 0, 0, 1, 3),
-    ("O", 2, 0),
-    ("C", 0, 0, 3, 4),
+    ("2", 0, 2, 0),
     ("T", 3, 0),
-    ("2", 0, 2, 0),
+    ("3", 0, 2, 0),
+    ("C", 0, 0, 0, 2),
     ("H", 0, 1, 0),
-    ("Gs", 0, 0, 5, 6),
     ("G", 1, 0),
-    ("Gs", 1, 0, 0, 2),
-    ("C", 0, 0, 4, 5),
+    ("Gs", 1, 0, 0, 1),
     ("O", 3, 0),
-    ("3", 0, 2, 0),
-    ("2", 0, 3, 0),
-    ("Gs", 1, 0, 2, 4),
     ("H", 0, 2, 0),
-    ("C", 0, 0, 5, 6),
-    ("C", 1, 0, 0, 3),
-    ("3", 0, 3, 0),
-    ("Gs", 1, 0, 4, 5),
     ("G", 2, 0),
+    ("C", 0, 0, 2, 3),
     ("Gs", 2, 0, 0, 1),
     ("D", 0, 0),
+    ("Gs", 1, 0, 1, 2),
+    ("2", 1, 0, 0),
+    ("2", 0, 3, 0),
+    ("C", 1, 0, 0, 1),
+    ("Gs", 1, 0, 2, 3),
+    ("C", 2, 0, 0, 1),
+    ("3", 0, 3, 0),
+    ("3", 1, 0, 0),
+    ("C", 1, 0, 1, 2),
+    ("Lo", 1),
+    ("C", 1, 0, 2, 3),
     ("Gs", 2, 0, 1, 2),
     ("H", 0, 3, 0),
-    ("Gs", 1, 0, 5, 6),
-    ("C", 1, 0, 3, 4),
-    ("2", 1, 0, 0),
-    ("Gs", 2, 0, 2, 3),
-    ("C", 2, 0, 0, 1),
-    ("C", 1, 0, 4, 5),
     ("G", 3, 0),
     ("Gs", 3, 0, 0, 1),
-    ("Lo", 1),
-    ("3", 1, 0, 0),
+    ("D", 1, 0),
+    ("Lq", 1),
+    ("2", 1, 1, 0),
     ("Gs", 3, 0, 1, 2),
+    ("H", 1, 0, 0),
+    ("3", 1, 1, 0),
+    ("Gs", 2, 0, 2, 3),
+    ("Gs", 3, 0, 2, 3),
+    ("C", 2, 0, 1, 3),
     ("C", 3, 0, 0, 1),
-    ("C", 1, 0, 5, 6),
-    ("C", 2, 0, 1, 2),
-    ("Gs", 2, 0, 3, 4),
-    ("C", 2, 0, 2, 3),
-    ("D", 1, 0),
-    ("Gs", 3, 0, 2, 4),
-    ("H", 1, 0, 0),
-    ("2", 1, 1, 0),
-    ("Gs", 2, 0, 4, 5),
+    ("Q", 0, 1),
     ("C", 3, 0, 1, 2),
-    ("3", 1, 1, 0),
-    ("Lq", 1),
-    ("Gs", 2, 0, 5, 6),
+    ("D", 2, 0),
+    ("H", 1, 1, 0),
+    ("2", 1, 2, 0),
     ("C", 3, 0, 2, 3),
-    ("Gs", 3, 0, 4, 5),
-    ("C", 3, 0, 3, 4),
-    ("C", 2, 0, 3, 4),
-    ("Q", 0, 1),
-    ("Gs", 3, 0, 5, 6),
-    ("C", 2, 0, 4, 5),
-    ("H", 1, 1, 0),
-    ("C", 2, 0, 5, 6),
-    ("Qs", 0, 1, 0, 4),
-    ("C", 3, 0, 4, 6),
-    ("Qs", 0, 1, 4, 6),
-    ("D", 2, 0),
     ("Q", 1, 1),
-    ("Qs", 1, 1, 0, 2),
-    ("2", 1, 2, 0),
-    ("Qs", 1, 1, 2, 4),
+    ("Qs", 0, 1, 0, 2),
     ("D", 3, 0),
-    ("S", 0, 1),
     ("3", 1, 2, 0),
     ("2", 1, 3, 0),
-    ("Qs", 1, 1, 4, 6),
+    ("Qs", 1, 1, 0, 2),
+    ("S", 0, 1),
     ("T", 0, 1),
     ("H", 1, 2, 0),
     ("Q", 2, 1),
-    ("Qs", 2, 1, 0, 2),
+    ("3", 1, 3, 0),
     ("S", 1, 1),
-    ("3", 1, 3, 0),
+    ("Qs", 2, 1, 0, 1),
     ("O", 0, 1),
-    ("Qs", 2, 1, 2, 6),
+    ("2", 0, 0, 1),
+    ("Qs", 2, 1, 1, 2),
+    ("H", 1, 3, 0),
     ("T", 1, 1),
-    ("2", 0, 0, 1),
-    ("H", 1, 3, 0),
     ("Q", 3, 1),
     ("Lg", 1),
     ("S", 2, 1),
+    ("3", 0, 0, 1),
     ("Qs", 3, 1, 0, 2),
-    ("3", 0, 0, 1),
-    ("Qs", 3, 1, 2, 4),
     ("O", 1, 1),
+    ("2", 0, 1, 1),
     ("T", 2, 1),
-    ("2", 0, 1, 1),
     ("H", 0, 0, 1),
-    ("Qs", 3, 1, 4, 6),
     ("G", 0, 1),
     ("Gs", 0, 1, 0, 1),
     ("3", 0, 1, 1),
     ("Gs", 0, 1, 1, 3),
+    ("O", 2, 1),
     ("S", 3, 1),
-    ("O", 2, 1),
     ("C", 0, 1, 0, 1),
     ("2", 0, 2, 1),
+    ("H", 0, 1, 1),
     ("T", 3, 1),
-    ("Gs", 0, 1, 3, 5),
-    ("H", 0, 1, 1),
+    ("C", 0, 1, 1, 2),
+    ("3", 0, 2, 1),
+    ("Ld", 1),
     ("G", 1, 1),
+    ("Gs", 1, 1, 0, 1),
+    ("C", 0, 1, 2, 3),
     ("O", 3, 1),
-    ("Gs", 1, 1, 0, 1),
-    ("3", 0, 2, 1),
-    ("Gs", 1, 1, 1, 3),
+    ("2", 0, 3, 1),
+    ("Gs", 1, 1, 1, 2),
     ("H", 0, 2, 1),
-    ("2", 0, 3, 1),
-    ("C", 0, 1, 1, 2),
     ("C", 1, 1, 0, 1),
-    ("Gs", 1, 1, 3, 4),
     ("G", 2, 1),
-    ("Gs", 1, 1, 4, 5),
     ("Gs", 2, 1, 0, 1),
-    ("Gs", 0, 1, 5, 6),
+    ("3", 0, 3, 1),
     ("Gs", 2, 1, 1, 2),
+    ("H", 0, 3, 1),
+    ("Gs", 1, 1, 2, 3),
     ("C", 1, 1, 1, 2),
-    ("3", 0, 3, 1),
+    ("C", 2, 1, 0, 1),
+    ("Gs", 2, 1, 2, 3),
+    ("G", 3, 1),
+    ("D", 0, 1),
+    ("C", 2, 1, 1, 2),
+    ("Gs", 3, 1, 0, 1),
     ("C", 1, 1, 2, 3),
-    ("C", 2, 1, 0, 1),
-    ("C", 1, 1, 3, 4),
-    ("H", 0, 3, 1),
-    ("C", 2, 1, 1, 2),
-    ("Gs", 2, 1, 2, 3),
-    ("Gs", 1, 1, 5, 6),
-    ("C", 0, 1, 2, 4),
-    ("Gs", 2, 1, 3, 4),
     ("C", 2, 1, 2, 3),
-    ("Gs", 2, 1, 4, 5),
-    ("C", 1, 1, 4, 5),
-    ("Gs", 2, 1, 5, 6),
-    ("C", 2, 1, 3, 4),
-    ("C", 0, 1, 4, 5),
-    ("G", 3, 1),
-    ("C", 0, 1, 5, 6),
-    ("C", 2, 1, 4, 5),
-    ("Gs", 3, 1, 0, 1),
-    ("C", 1, 1, 5, 6),
-    ("Gs", 3, 1, 1, 2),
-    ("Ld", 1),
+    ("Gs", 3, 1, 1, 3),
+    ("D", 2, 1),
+    ("D", 1, 1),
     ("C", 3, 1, 0, 1),
-    ("Gs", 3, 1, 2, 3),
-    ("D", 0, 1),
-    ("C", 2, 1, 5, 6),
-    ("Gs", 3, 1, 3, 4),
-    ("D", 1, 1),
-    ("C", 3, 1, 1, 2),
-    ("Gs", 3, 1, 4, 6),
     ("2", 1, 0, 1),
-    ("C", 3, 1, 2, 3),
     ("2", 1, 1, 1),
-    ("C", 3, 1, 3, 5),
-    ("D", 2, 1),
-    ("C", 3, 1, 5, 6),
+    ("C", 3, 1, 1, 3),
     ("2", 1, 2, 1),
     ("D", 3, 1),
+    ("3", 1, 0, 1),
+    ("3", 1, 1, 1),
     ("2", 1, 3, 1),
-    ("3", 1, 0, 1),
+    ("H", 1, 1, 1),
     ("3", 1, 2, 1),
+    ("3", 1, 3, 1),
+    ("H", 1, 2, 1),
     ("H", 1, 0, 1),
-    ("3", 1, 1, 1),
-    ("3", 1, 3, 1),
-    ("H", 1, 1, 1),
-    ("H", 1, 2, 1),
     ("H", 1, 3, 1),
 ]
 
@@ -330,8 +287,13 @@
     start(wo_loads(0))
     start(wd_loads(0))
 
-    def tile_copy(m, j, n, c0, w):
-        return rc(GP.at[m, j, oy, :, pl.ds(c0, w)], GR.at[m, j, :, pl.ds(c0, w)], g_ss.at[m, j, n], g_rs.at[m, j, n], ypeer)
+    def q_copy(m, n):
+        cols = pl.ds(0, (2 * QW, QW)[n])
+        return rc(GP.at[m, n, oy, :, cols], GR.at[m, n, :, cols], g_ss.at[m, n], g_rs.at[m, n], ypeer)
+
+    def g_copy(m, n):
+        cols = pl.ds(*GU_SENDS[n])
+        return rc(GP.at[m, :, oy, :, cols], GR.at[m, :, :, cols], g_ss.at[m, n], g_rs.at[m, n], ypeer)
 
     def compute_tile(m, j, c0, w, transposed=False):
         xm = X[m].reshape(2 * R, DW)
@@ -353,8 +315,8 @@
             lax.fori_loop(0, cnt, body, 0)
 
     def send_q(m, lo, hi):
-        for j, c0 in QKV_TILES[lo:hi]:
-            tile_copy(m, j, c0 // TW, c0, TW).start()
+        for n in range(lo, hi):
+            q_copy(m, n).start()
 
     def phase_g(m):
         def body(i, _):
@@ -366,15 +328,8 @@
             compute_tile(m, j, 2560, 192, True)
 
     def send_g(m, lo, hi):
-        def body(n, _):
-            for j in range(2):
-                tile_copy(m, j, n, pl.multiple_of(n * TW, TW), TW).start()
-            return 0
-        if lo < 5:
-            lax.fori_loop(lo, min(hi, 5), body, 0)
-        if hi == 6:
-            for j in range(2):
-                tile_copy(m, j, 5, 2560, 256).start()
+        for n in range(lo, hi):
+            g_copy(m, n).start()
 
     def stat_copies(kind, m):
         peers = (cpeer, xpeer, xdiag) if kind == 0 else (cpeer, ypeer, ydiag)
@@ -398,8 +353,8 @@
         RSC[1] = jnp.broadcast_to(scale[0:R, 1:2], (R, 128))
 
     def phase_s(m):
-        for n, (j, c0) in enumerate(QKV_TILES):
-            tile_copy(m, j, c0 // TW, c0, TW).wait()
+        for n in range(2):
+            q_copy(m, n).wait()
 
         def body(i, _):
             rows = pl.ds(pl.multiple_of(i * 16, 16), 16)
@@ -510,8 +465,8 @@
                 p_copy(m).start()
 
     def phase_d(m, l):
-        for n, (c0, w) in enumerate(GU_TILES):
-            c_copy(m, n, c0, w).wait()
+        for n in range(3):
+            c_copy(m, n).wait()
         for half in (1 - core, core):
             def body(i, _):
                 cols = pl.ds(pl.multiple_of(half * HALF + i * TW, TW), TW)
@@ -561,31 +516,23 @@
             return 0
         lax.fori_loop(0, 2 * R // 16, body, 0)
 
-    def c_copy(m, n, c0, w):
-        return rc(C.at[m, ty, :, pl.ds(c0, w)], C.at[m, ty, :, pl.ds(c0, w)], c_ss.at[m, n], c_rs.at[m, n], ypeer)
-
-    def c_tile(m, n, c0, w):
-        for j in range(2):
-            tile_copy(m, j, n, c0, w).wait()
-
-        def body(i, _):
-            rows = pl.ds(pl.multiple_of(i * 16, 16), 16)
-            cols = pl.ds(c0, w)
-            g = (GP[m, 0, ty, rows, cols].astype(F32) + GR[m, 0, rows, cols].astype(F32)).astype(BF).astype(F32)
-            u = (GP[m, 1, ty, rows, cols].astype(F32) + GR[m, 1, rows, cols].astype(F32)).astype(BF).astype(F32)
-            C[m, ty, rows, cols] = (jax.nn.silu(g) * u).astype(BF)
-            return 0
-        lax.fori_loop(0, R // 16, body, 0)
-        c_copy(m, n, c0, w).start()
+    def c_copy(m, n):
+        cols = pl.ds(*GU_SENDS[n])
+        return rc(C.at[m, ty, :, cols], C.at[m, ty, :, cols], c_ss.at[m, n], c_rs.at[m, n], ypeer)
 
     def phase_c(m, lo, hi):
-        def body(n, _):
-            c_tile(m, n, pl.multiple_of(n * TW, TW), TW)
-            return 0
-        if lo < 5:
-            lax.fori_loop(lo, min(hi, 5), body, 0)
-        if hi == 6:
-            c_tile(m, 5, 2560, 256)
+        for n in range(lo, hi):
+            g_copy(m, n).wait()
+
+            def body(i, _):
+                rows = pl.ds(pl.multiple_of(i * 16, 16), 16)
+                cols = pl.ds(*GU_SENDS[n])
+                g = (GP[m, 0, ty, rows, cols].astype(F32) + GR[m, 0, rows, cols].astype(F32)).astype(BF).astype(F32)
+                u = (GP[m, 1, ty, rows, cols].astype(F32) + GR[m, 1, rows, cols].astype(F32)).astype(BF).astype(F32)
+                C[m, ty, rows, cols] = (jax.nn.silu(g) * u).astype(BF)
+                return 0
+            lax.fori_loop(0, R // 16, body, 0)
+            c_copy(m, n).start()
 
     def y_copies(m):
         out = []
@@ -724,7 +671,7 @@
                 pltpu.VMEM((3, NB, 8, 128), F32),
                 pltpu.VMEM((3, NB, 3, 8, 128), F32),
                 dma((NB * 2 * T,)), dma((6,)), dma((8,)), dma((1,)), dma((4,)), dma((2, SLOTS)), dma((2, NB)), dma((NB * 2 * T,)),
-                dma((NB, 2, 6)), dma((NB, 2, 6)), dma((NB, 6)), dma((NB, 6)), dma((NB,)), dma((NB,)),
+                dma((NB, 3)), dma((NB, 3)), dma((NB, 3)), dma((NB, 3)), dma((NB,)), dma((NB,)),
                 dma((NB,)), dma((NB,)), dma((NB,)), dma((2, NB)), dma((NB,)), dma((NB,)), dma((3, NB, 3)), dma((3, NB, 3)),
             ],
             compiler_params=pltpu.CompilerParams(collective_id=0, has_side_effects=True, vmem_limit_bytes=67043328),

time: 343 us -> 338 us (0.985)
  Pallas kernels: 338 us -> 333 us
    pallas_call x1, Pallas kernels: 310 us -> 305 us  [device_fn(): pl.pallas_call(main_kernel, out_shape=[jax.ShapeDtypeStruct(embeds.shape,...]
where the time goes in v5:
time: 338 us
  Pallas kernels  333 us (99%)
    pallas_call x1, Pallas kernels, device_fn(): pl.pallas_call(main_kernel, out_shape=[jax.ShapeDtypeStruct(embeds.shape,...  305 us
    pallas_call x1, Pallas kernels, device_fn(): pl.pallas_call(cache_kernel, out_shape=[jax.ShapeDtypeStruct(k_cache.shap...  27.9 us

profile of v5, /device:TPU:0, one launch (start us, length us, event | category | flops | bytes accessed | tf_op | source)
XLA Modules:
  0.0 337.8 jit_solution(3727016441049354061)
XLA Ops:
  0.6 0.7 dynamic_slice.3.start_ref
  1.4 0.0 copy-start.1
  1.4 0.6 copy-done.1
  1.9 0.1 add.30
  2.0 0.1 add.34
  2.1 0.1 add.32
  2.2 0.4 fusion
  2.7 0.8 pad_maximum_fusion
  3.4 305.3 %layers.1 = (bf16[3,128,2048]{2,1,0:T(8,128)(2,1)}, bf16[2,64,24,128]{3,2,1,0:T(8,128)(2,1)}, bf16[2,64,24,128]{3,2,1,0:T(8,128)(2,1)}) custom-call(s32[64]{0:T(128)} %copy-done.1, bf16[3,128,2048]{2,1,0:T(8,128)(2,1)} %emb_ref.1, bf16[2,64,512,128]{3,2,1,0:T(8,128)(2,1)} %bitcast.6, bf16[2,64,512,128]{3,2,1,0:T(8,128)(2,1)} %bitcast.7, ...), custom_call_target="tpu_custom_call" | custom-call | tf_op jit(solution)/shard_map/layers/pallas_call | solution.py:638
  308.7 0.0 copy-start
  308.7 27.9 %caches.1 = (bf16[2,64,64,8,128]{4,3,2,1,0:T(8,128)(2,1)}, bf16[2,64,64,8,128]{4,3,2,1,0:T(8,128)(2,1)}) custom-call(s32[64]{0:T(128)} %copy-done.1, bf16[2,64,64,8,128]{4,3,2,1,0:T(8,128)(2,1)} %k_ref.1, bf16[2,64,64,8,128]{4,3,2,1,0:T(8,128)(2,1)} %v_ref.1, bf16[2,64,3,8,128]{4,3,2,1,0:T(8,128)(2,1)} %bitcast.10, bf16[2,64,3,8,128]{4,3,2,1,0:T(8,128)(2,1)} %bitcast.11), custom_call_target="tpu_custom_call" | custom-call | tf_op jit(solution)/shard_map/caches/pallas_call | solution.py:684
  336.6 0.0 copy-done
  336.6 1.1 copy.19
  (4 shorter events, 0.0 us)
Async XLA Ops:
  1.4 0.6 copy-start.1
  308.7 27.9 %copy-start = (bf16[3,128,2048]{2,1,0:T(8,128)(2,1)S(1)}, bf16[3,128,2048]{2,1,0:T(8,128)(2,1)}, u32[]{:S(2)}) copy-start(bf16[3,128,2048]{2,1,0:T(8,128)(2,1)} %get-tuple-element.21) | copy-start | bytes 4718596

commit v6 on v5

--- a/solution.py
+++ b/solution.py
@@ -40,160 +40,160 @@
 
 ORDER = [
     ("Q", 0, 0),
-    ("Qs", 0, 0, 0, 1),
+    ("Qs", 0, 0, 0, 2),
+    ("Q", 2, 0),
     ("Q", 1, 0),
-    ("Qs", 0, 0, 1, 2),
     ("Qs", 1, 0, 0, 1),
-    ("Q", 2, 0),
+    ("Q", 3, 0),
     ("S", 0, 0),
     ("Qs", 1, 0, 1, 2),
+    ("Lg", 0),
+    ("Qs", 2, 0, 0, 1),
     ("T", 0, 0),
-    ("Q", 3, 0),
-    ("Qs", 2, 0, 0, 1),
     ("S", 1, 0),
     ("Qs", 2, 0, 1, 2),
+    ("T", 1, 0),
     ("O", 0, 0),
+    ("S", 2, 0),
     ("2", 0, 0, 0),
-    ("Lg", 0),
-    ("T", 1, 0),
-    ("Qs", 3, 0, 0, 1),
-    ("S", 2, 0),
+    ("T", 2, 0),
     ("O", 1, 0),
     ("3", 0, 0, 0),
-    ("T", 2, 0),
+    ("2", 0, 1, 0),
+    ("Qs", 3, 0, 0, 1),
+    ("H", 0, 0, 0),
     ("Qs", 3, 0, 1, 2),
-    ("H", 0, 0, 0),
     ("G", 0, 0),
     ("Gs", 0, 0, 0, 1),
-    ("O", 2, 0),
-    ("2", 0, 1, 0),
-    ("Gs", 0, 0, 1, 3),
     ("S", 3, 0),
     ("3", 0, 1, 0),
+    ("O", 2, 0),
+    ("Gs", 0, 0, 1, 2),
+    ("T", 3, 0),
+    ("H", 0, 1, 0),
     ("2", 0, 2, 0),
-    ("T", 3, 0),
+    ("C", 0, 0, 0, 1),
+    ("Gs", 0, 0, 2, 3),
+    ("C", 0, 0, 1, 2),
+    ("G", 1, 0),
+    ("C", 0, 0, 2, 3),
     ("3", 0, 2, 0),
-    ("C", 0, 0, 0, 2),
-    ("H", 0, 1, 0),
-    ("G", 1, 0),
-    ("Gs", 1, 0, 0, 1),
     ("O", 3, 0),
+    ("Gs", 1, 0, 0, 3),
     ("H", 0, 2, 0),
+    ("2", 0, 3, 0),
     ("G", 2, 0),
-    ("C", 0, 0, 2, 3),
+    ("C", 1, 0, 0, 1),
     ("Gs", 2, 0, 0, 1),
+    ("C", 1, 0, 1, 2),
+    ("3", 0, 3, 0),
+    ("C", 1, 0, 2, 3),
     ("D", 0, 0),
-    ("Gs", 1, 0, 1, 2),
     ("2", 1, 0, 0),
-    ("2", 0, 3, 0),
-    ("C", 1, 0, 0, 1),
-    ("Gs", 1, 0, 2, 3),
+    ("Gs", 2, 0, 1, 3),
     ("C", 2, 0, 0, 1),
-    ("3", 0, 3, 0),
+    ("H", 0, 3, 0),
     ("3", 1, 0, 0),
-    ("C", 1, 0, 1, 2),
-    ("Lo", 1),
-    ("C", 1, 0, 2, 3),
-    ("Gs", 2, 0, 1, 2),
-    ("H", 0, 3, 0),
     ("G", 3, 0),
+    ("C", 2, 0, 1, 2),
     ("Gs", 3, 0, 0, 1),
+    ("Lq", 1),
     ("D", 1, 0),
-    ("Lq", 1),
     ("2", 1, 1, 0),
+    ("H", 1, 0, 0),
+    ("C", 2, 0, 2, 3),
     ("Gs", 3, 0, 1, 2),
-    ("H", 1, 0, 0),
+    ("Q", 0, 1),
+    ("Qs", 0, 1, 0, 1),
+    ("D", 2, 0),
+    ("2", 1, 2, 0),
     ("3", 1, 1, 0),
-    ("Gs", 2, 0, 2, 3),
+    ("Qs", 0, 1, 1, 2),
     ("Gs", 3, 0, 2, 3),
-    ("C", 2, 0, 1, 3),
     ("C", 3, 0, 0, 1),
-    ("Q", 0, 1),
+    ("H", 1, 1, 0),
+    ("S", 0, 1),
     ("C", 3, 0, 1, 2),
-    ("D", 2, 0),
-    ("H", 1, 1, 0),
-    ("2", 1, 2, 0),
+    ("3", 1, 2, 0),
+    ("Q", 1, 1),
     ("C", 3, 0, 2, 3),
-    ("Q", 1, 1),
-    ("Qs", 0, 1, 0, 2),
-    ("D", 3, 0),
-    ("3", 1, 2, 0),
-    ("2", 1, 3, 0),
     ("Qs", 1, 1, 0, 2),
-    ("S", 0, 1),
     ("T", 0, 1),
     ("H", 1, 2, 0),
+    ("D", 3, 0),
+    ("2", 1, 3, 0),
+    ("Lo", 1),
     ("Q", 2, 1),
+    ("Qs", 2, 1, 0, 1),
+    ("S", 1, 1),
+    ("O", 0, 1),
     ("3", 1, 3, 0),
-    ("S", 1, 1),
-    ("Qs", 2, 1, 0, 1),
-    ("O", 0, 1),
+    ("Qs", 2, 1, 1, 2),
+    ("T", 1, 1),
     ("2", 0, 0, 1),
-    ("Qs", 2, 1, 1, 2),
     ("H", 1, 3, 0),
-    ("T", 1, 1),
     ("Q", 3, 1),
     ("Lg", 1),
     ("S", 2, 1),
+    ("O", 1, 1),
     ("3", 0, 0, 1),
-    ("Qs", 3, 1, 0, 2),
-    ("O", 1, 1),
+    ("Qs", 3, 1, 0, 1),
+    ("T", 2, 1),
+    ("Qs", 3, 1, 1, 2),
     ("2", 0, 1, 1),
-    ("T", 2, 1),
     ("H", 0, 0, 1),
     ("G", 0, 1),
+    ("Ld", 1),
     ("Gs", 0, 1, 0, 1),
-    ("3", 0, 1, 1),
-    ("Gs", 0, 1, 1, 3),
     ("O", 2, 1),
     ("S", 3, 1),
+    ("Gs", 0, 1, 1, 2),
+    ("3", 0, 1, 1),
+    ("2", 0, 2, 1),
+    ("T", 3, 1),
     ("C", 0, 1, 0, 1),
-    ("2", 0, 2, 1),
+    ("3", 0, 2, 1),
+    ("C", 0, 1, 1, 2),
+    ("Gs", 0, 1, 2, 3),
     ("H", 0, 1, 1),
-    ("T", 3, 1),
-    ("C", 0, 1, 1, 2),
-    ("3", 0, 2, 1),
-    ("Ld", 1),
     ("G", 1, 1),
-    ("Gs", 1, 1, 0, 1),
-    ("C", 0, 1, 2, 3),
+    ("Gs", 1, 1, 0, 3),
     ("O", 3, 1),
     ("2", 0, 3, 1),
-    ("Gs", 1, 1, 1, 2),
     ("H", 0, 2, 1),
-    ("C", 1, 1, 0, 1),
     ("G", 2, 1),
     ("Gs", 2, 1, 0, 1),
+    ("C", 1, 1, 0, 1),
     ("3", 0, 3, 1),
     ("Gs", 2, 1, 1, 2),
+    ("C", 0, 1, 2, 3),
     ("H", 0, 3, 1),
-    ("Gs", 1, 1, 2, 3),
-    ("C", 1, 1, 1, 2),
+    ("C", 1, 1, 1, 3),
     ("C", 2, 1, 0, 1),
+    ("G", 3, 1),
     ("Gs", 2, 1, 2, 3),
-    ("G", 3, 1),
+    ("Gs", 3, 1, 0, 1),
     ("D", 0, 1),
     ("C", 2, 1, 1, 2),
-    ("Gs", 3, 1, 0, 1),
-    ("C", 1, 1, 2, 3),
+    ("Gs", 3, 1, 1, 2),
+    ("D", 1, 1),
+    ("2", 1, 0, 1),
     ("C", 2, 1, 2, 3),
-    ("Gs", 3, 1, 1, 3),
+    ("2", 1, 1, 1),
+    ("Gs", 3, 1, 2, 3),
+    ("C", 3, 1, 0, 2),
     ("D", 2, 1),
-    ("D", 1, 1),
-    ("C", 3, 1, 0, 1),
-    ("2", 1, 0, 1),
-    ("2", 1, 1, 1),
-    ("C", 3, 1, 1, 3),
     ("2", 1, 2, 1),
-    ("D", 3, 1),
+    ("C", 3, 1, 2, 3),
     ("3", 1, 0, 1),
     ("3", 1, 1, 1),
+    ("D", 3, 1),
     ("2", 1, 3, 1),
     ("H", 1, 1, 1),
+    ("H", 1, 0, 1),
     ("3", 1, 2, 1),
     ("3", 1, 3, 1),
     ("H", 1, 2, 1),
-    ("H", 1, 0, 1),
     ("H", 1, 3, 1),
 ]
 
@@ -375,14 +375,14 @@
         stat_recv(0, m)
 
         gain = jnp.concatenate([qg_ref[pl.ds(l, 1)], kg_ref[pl.ds(l, 1)]], axis=1).astype(F32)
-        low = lax.rem(lax.broadcasted_iota(jnp.int32, (16, 2 * QW), 1), HEAD_DIM) < HEAD_DIM // 2
+        low = lax.rem(lax.broadcasted_iota(jnp.int32, (RB, 2 * QW), 1), HEAD_DIM) < HEAD_DIM // 2
 
         def body(i, _):
-            rows = pl.ds(pl.multiple_of(i * 16, 16), 16)
+            rows = pl.ds(pl.multiple_of(i * RB, RB), RB)
             scale = jnp.concatenate([RSC[0, rows]] * HL + [RSC[1, rows]] * HL, axis=1)
             z = GR[m, 0, rows, pl.ds(0, 2 * QW)].astype(F32) * scale * gain
             turned = jnp.where(low, pltpu.roll(z, 2 * QW - HEAD_DIM // 2, 1), pltpu.roll(z, HEAD_DIM // 2, 1))
-            rot = z * jnp.concatenate([cos_ref[m, rows]] * (2 * HL), axis=1) + turned * jnp.concatenate([sin_ref[m, rows]] * (2 * HL), axis=1)
+            rot = z * jnp.concatenate([cos_ref[ty, m, rows]] * (2 * HL), axis=1) + turned * jnp.concatenate([sin_ref[ty, m, rows]] * (2 * HL), axis=1)
             rot = rot.astype(BF).astype(F32)
             v = GR[m, 1, rows, pl.ds(0, QW)].astype(F32)
             for h in range(HL):
@@ -390,7 +390,7 @@
                 KS[i, :, h, :] = rot[:, QW + h * HEAD_DIM:QW + (h + 1) * HEAD_DIM]
                 VS[i, :, h, :] = v[:, h * HEAD_DIM:(h + 1) * HEAD_DIM]
             return 0
-        lax.fori_loop(0, R // 16, body, 0)
+        lax.fori_loop(0, T, body, 0)
 
     def ko_copies(l, m):
         rows = pl.ds(m * RB, RB)
@@ -412,14 +412,14 @@
         nxt = (l, m + 1) if m + 1 < NB else (l + 1, 0)
 
         def chunk(c, _):
-            slot = c
+            slot = lax.rem(c, SLOTS)
             wait(kv_copies(l, m, c, slot))
             for k in range(CB):
                 i = c * CB + k
                 q = QS[:, i].reshape(T * HL, HEAD_DIM).astype(BF)
                 kn = KS[:, i].reshape(T * HL, HEAD_DIM).astype(BF)
                 vn = VS[:, i].reshape(T * HL, HEAD_DIM).astype(BF)
-                limit = start_ref[m * RB + i] * HL
+                limit = start_ref[ty * NB * RB + m * RB + i] * HL
                 s_old = jnp.where(colm < limit, dot_t(q, KB[slot, k]) * SCORE_SCALE, NEG_BIG)
                 s_new = jnp.where(newm, dot_t(q, kn) * SCORE_SCALE, NEG_BIG)
                 top = jnp.maximum(jnp.max(s_old, axis=1, keepdims=True), jnp.max(s_new, axis=1, keepdims=True))
@@ -430,18 +430,25 @@
                 OS[:, i] = o.reshape(T, HL, HEAD_DIM)
                 KO[m, i] = kn
                 VO[m, i] = vn
+            if NCH > SLOTS:
+                @pl.when(c < NCH - SLOTS)
+                def _():
+                    start(kv_copies(l, m, c + SLOTS, slot))
+
             if nxt[0] < L:
-                start(kv_copies(nxt[0], nxt[1], c, slot))
+                @pl.when(c >= NCH - SLOTS)
+                def _():
+                    start(kv_copies(nxt[0], nxt[1], c - (NCH - SLOTS), slot))
             return 0
         lax.fori_loop(0, NCH, chunk, 0)
         start(ko_copies(l, m))
 
         def body(i, _):
-            rows = pl.ds(pl.multiple_of(i * 16, 16), 16)
+            rows = pl.ds(pl.multiple_of(i * RB, RB), RB)
             for h in range(8):
                 OB[m, ty, rows, pl.ds(h * 128, 128)] = OS[i, :, h, :].astype(BF)
             return 0
-        lax.fori_loop(0, R // 16, body, 0)
+        lax.fori_loop(0, T, body, 0)
         o_copy(m).start()
 
     def p_copy(m):
@@ -606,10 +613,11 @@
 
 def cache_kernel(start_ref, k_ref, v_ref, kn_ref, vn_ref, ko_ref, vo_ref):
     c = pl.program_id(1)
+    base = lax.axis_index("tpy") * NB * RB + c * k_ref.shape[1]
     ko_ref[...] = k_ref[...]
     vo_ref[...] = v_ref[...]
     for i in range(k_ref.shape[1]):
-        p = start_ref[c * k_ref.shape[1] + i]
+        p = start_ref[base + i]
         for t in range(T):
             ko_ref[0, i, p + t] = kn_ref[0, i, t]
             vo_ref[0, i, p + t] = vn_ref[0, i, t]
@@ -625,8 +633,7 @@
 
     def device_fn(embeds, start_pos, k_cache, v_cache, w_query, w_key, w_value, w_out, w_gate, w_up, w_down, q_gain, k_gain, attn_gain, mlp_gain):
         rows = NB * RB
-        start_local = lax.dynamic_slice_in_dim(start_pos, lax.axis_index('tpy') * rows, rows)
-        pos = (start_local.reshape(NB, 1, RB) + jnp.arange(T, dtype=jnp.int32)[None, :, None]).reshape(NB, R)
+        pos = (start_pos.reshape(2, NB, 1, RB) + jnp.arange(T, dtype=jnp.int32)[None, None, :, None]).reshape(2, NB, R)
         inv_freq = jnp.power(THETA, jnp.arange(HEAD_DIM // 2, dtype=F32) * (-2.0 / HEAD_DIM))
         ang = pos.astype(F32)[..., None] * inv_freq
         cos_part, sin_part = jnp.cos(ang), jnp.sin(ang)
@@ -676,9 +683,9 @@
             ],
             compiler_params=pltpu.CompilerParams(collective_id=0, has_side_effects=True, vmem_limit_bytes=67043328),
             name="layers",
-        )(start_local, embeds, k_cache.reshape(L, rows, SH, HEAD_DIM), v_cache.reshape(L, rows, SH, HEAD_DIM),
+        )(start_pos, embeds, k_cache.reshape(L, rows, SH, HEAD_DIM), v_cache.reshape(L, rows, SH, HEAD_DIM),
           w_query, w_key, w_value, w_out, w_gate.transpose(0, 2, 1), w_up.transpose(0, 2, 1), w_down, q_gain, k_gain, attn_gain, mlp_gain, cos2, sin2)
-        bc = 8
+        bc = 16
         big = pl.BlockSpec((1, bc, SEQ, HL, HEAD_DIM), lambda l, c, s: (l, c, 0, 0, 0))
         small = pl.BlockSpec((1, bc, T, HL, HEAD_DIM), lambda l, c, s: (l, c, 0, 0, 0))
         k_out, v_out = pl.pallas_call(
@@ -686,8 +693,9 @@
             out_shape=[jax.ShapeDtypeStruct(k_cache.shape, BF)] * 2,
             grid_spec=pltpu.PrefetchScalarGridSpec(
                 num_scalar_prefetch=1, grid=(L, rows // bc), in_specs=[big, big, small, small], out_specs=[big, big]),
+            compiler_params=pltpu.CompilerParams(vmem_limit_bytes=48 * 1024 * 1024),
             name="caches",
-        )(start_local, k_cache, v_cache, kn.reshape(L, rows, T, HL, HEAD_DIM), vn.reshape(L, rows, T, HL, HEAD_DIM))
+        )(start_pos, k_cache, v_cache, kn.reshape(L, rows, T, HL, HEAD_DIM), vn.reshape(L, rows, T, HL, HEAD_DIM))
         return y, k_out, v_out
 
     return jax.shard_map(device_fn, mesh=mesh, in_specs=(act_spec, P('dp'), cache_spec, cache_spec, col_spec, col_spec, col_spec, row_spec, col_spec, col_spec, row_spec, head_gain, head_gain, width_gain, width_gain), out_specs=(act_spec, cache_spec, cache_spec), check_vma=False)

time: 338 us -> 312 us (0.923)
  Pallas kernels: 333 us -> 304 us
    pallas_call x1, Pallas kernels: 305 us -> 281 us  [device_fn(): pl.pallas_call(main_kernel, out_shape=[jax.ShapeDtypeStruct(embeds.shape,...]
    pallas_call x1, Pallas kernels: 27.9 us -> 23.2 us  [device_fn(): pl.pallas_call(cache_kernel, out_shape=[jax.ShapeDtypeStruct(k_cache.shap...]
where the time goes in v6:
time: 312 us
  Pallas kernels  304 us (97%)
  local copies, waits for them, and re-layouts  4.98 us (2%)
    pallas_call x1, Pallas kernels, device_fn(): pl.pallas_call(main_kernel, out_shape=[jax.ShapeDtypeStruct(embeds.shape,...  281 us
    pallas_call x1, Pallas kernels, device_fn(): pl.pallas_call(cache_kernel, out_shape=[jax.ShapeDtypeStruct(k_cache.shap...  23.2 us

profile of v6, /device:TPU:0, one launch (start us, length us, event | category | flops | bytes accessed | tf_op | source)
XLA Modules:
  0.0 311.7 jit_solution(1601493236117327713)
XLA Ops:
  0.7 0.1 add.30
  0.7 0.7 add.26
  1.5 0.1 add.28
  1.6 0.8 fusion
  2.4 0.9 pad_maximum_fusion
  3.3 281.1 %layers.1 = (bf16[3,128,2048]{2,1,0:T(8,128)(2,1)}, bf16[2,64,24,128]{3,2,1,0:T(8,128)(2,1)}, bf16[2,64,24,128]{3,2,1,0:T(8,128)(2,1)}) custom-call(s32[128]{0:T(128)} %start_ref.3, bf16[3,128,2048]{2,1,0:T(8,128)(2,1)} %emb_ref.1, bf16[2,64,512,128]{3,2,1,0:T(8,128)(2,1)} %bitcast.8, bf16[2,64,512,128]{3,2,1,0:T(8,128)(2,1)} %bitcast.9, ...), custom_call_target="tpu_custom_call" | custom-call | tf_op jit(solution)/shard_map/layers/pallas_call | solution.py:645
  284.4 0.0 copy-start
  284.4 1.1 copy-done
  285.5 0.0 copy-start.1
  285.5 1.1 copy-done.1
  286.6 0.0 copy-start.2
  286.6 0.7 copy-done.2
  287.3 0.0 copy-start.3
  287.3 23.2 %caches.1 = (bf16[2,64,64,8,128]{4,3,2,1,0:T(8,128)(2,1)}, bf16[2,64,64,8,128]{4,3,2,1,0:T(8,128)(2,1)}) custom-call(s32[128]{0:T(128)S(1)} %copy-done.2, bf16[2,64,64,8,128]{4,3,2,1,0:T(8,128)(2,1)} %k_ref.1, bf16[2,64,64,8,128]{4,3,2,1,0:T(8,128)(2,1)} %v_ref.1, bf16[2,64,3,8,128]{4,3,2,1,0:T(8,128)(2,1)S(1)} %bitcast.6, ...), custom_call_target="tpu_custom_call" | custom-call | tf_op jit(solution)/shard_map/caches/pallas_call | solution.py:691
  310.5 0.0 copy-done.3
  310.5 1.1 copy.19
  (4 shorter events, 0.0 us)
Async XLA Ops:
  284.4 1.1 copy-start
  285.5 1.1 copy-start.1
  286.6 0.7 copy-start.2
  287.3 23.2 %copy-start.3 = (bf16[3,128,2048]{2,1,0:T(8,128)(2,1)S(1)}, bf16[3,128,2048]{2,1,0:T(8,128)(2,1)}, u32[]{:S(2)}) copy-start(bf16[3,128,2048]{2,1,0:T(8,128)(2,1)} %get-tuple-element.21) | copy-start | bytes 4718596

commit v7 on v6

--- a/solution.py
+++ b/solution.py
@@ -38,162 +38,164 @@
 QKV_TILES = [(0, 0), (0, 512), (0, 1024), (0, 1536), (1, 0), (1, 512)]
 
 
+Q_ROWS = (2, 1)
+G_ROWS = 1
 ORDER = [
     ("Q", 0, 0),
     ("Qs", 0, 0, 0, 2),
     ("Q", 2, 0),
-    ("Q", 1, 0),
     ("Qs", 1, 0, 0, 1),
-    ("Q", 3, 0),
     ("S", 0, 0),
     ("Qs", 1, 0, 1, 2),
-    ("Lg", 0),
     ("Qs", 2, 0, 0, 1),
     ("T", 0, 0),
+    ("Qs", 2, 0, 1, 2),
+    ("Qs", 3, 0, 0, 1),
     ("S", 1, 0),
-    ("Qs", 2, 0, 1, 2),
     ("T", 1, 0),
+    ("Qs", 3, 0, 1, 2),
     ("O", 0, 0),
     ("S", 2, 0),
+    ("Lg", 0),
     ("2", 0, 0, 0),
     ("T", 2, 0),
     ("O", 1, 0),
     ("3", 0, 0, 0),
     ("2", 0, 1, 0),
-    ("Qs", 3, 0, 0, 1),
+    ("S", 3, 0),
     ("H", 0, 0, 0),
-    ("Qs", 3, 0, 1, 2),
     ("G", 0, 0),
     ("Gs", 0, 0, 0, 1),
-    ("S", 3, 0),
+    ("O", 2, 0),
     ("3", 0, 1, 0),
-    ("O", 2, 0),
     ("Gs", 0, 0, 1, 2),
     ("T", 3, 0),
-    ("H", 0, 1, 0),
     ("2", 0, 2, 0),
     ("C", 0, 0, 0, 1),
     ("Gs", 0, 0, 2, 3),
-    ("C", 0, 0, 1, 2),
+    ("H", 0, 1, 0),
     ("G", 1, 0),
-    ("C", 0, 0, 2, 3),
+    ("Gs", 1, 0, 0, 1),
     ("3", 0, 2, 0),
     ("O", 3, 0),
-    ("Gs", 1, 0, 0, 3),
+    ("2", 0, 3, 0),
+    ("C", 0, 0, 1, 3),
+    ("C", 1, 0, 0, 1),
+    ("Gs", 1, 0, 1, 3),
     ("H", 0, 2, 0),
-    ("2", 0, 3, 0),
     ("G", 2, 0),
-    ("C", 1, 0, 0, 1),
+    ("3", 0, 3, 0),
     ("Gs", 2, 0, 0, 1),
-    ("C", 1, 0, 1, 2),
-    ("3", 0, 3, 0),
-    ("C", 1, 0, 2, 3),
     ("D", 0, 0),
     ("2", 1, 0, 0),
-    ("Gs", 2, 0, 1, 3),
+    ("Gs", 2, 0, 1, 2),
+    ("C", 1, 0, 1, 3),
+    ("H", 0, 3, 0),
+    ("Gs", 2, 0, 2, 3),
+    ("G", 3, 0),
     ("C", 2, 0, 0, 1),
-    ("H", 0, 3, 0),
     ("3", 1, 0, 0),
-    ("G", 3, 0),
-    ("C", 2, 0, 1, 2),
     ("Gs", 3, 0, 0, 1),
+    ("C", 2, 0, 1, 3),
+    ("Gs", 3, 0, 1, 2),
+    ("D", 1, 0),
     ("Lq", 1),
-    ("D", 1, 0),
+    ("H", 1, 0, 0),
     ("2", 1, 1, 0),
-    ("H", 1, 0, 0),
-    ("C", 2, 0, 2, 3),
-    ("Gs", 3, 0, 1, 2),
     ("Q", 0, 1),
+    ("3", 1, 1, 0),
     ("Qs", 0, 1, 0, 1),
     ("D", 2, 0),
-    ("2", 1, 2, 0),
-    ("3", 1, 1, 0),
     ("Qs", 0, 1, 1, 2),
     ("Gs", 3, 0, 2, 3),
-    ("C", 3, 0, 0, 1),
     ("H", 1, 1, 0),
+    ("2", 1, 2, 0),
+    ("C", 3, 0, 0, 2),
+    ("Q", 1, 1),
     ("S", 0, 1),
-    ("C", 3, 0, 1, 2),
+    ("C", 3, 0, 2, 3),
     ("3", 1, 2, 0),
-    ("Q", 1, 1),
-    ("C", 3, 0, 2, 3),
-    ("Qs", 1, 1, 0, 2),
+    ("Qs", 1, 1, 0, 1),
+    ("Lo", 1),
+    ("Qs", 1, 1, 1, 2),
     ("T", 0, 1),
-    ("H", 1, 2, 0),
     ("D", 3, 0),
     ("2", 1, 3, 0),
-    ("Lo", 1),
+    ("H", 1, 2, 0),
     ("Q", 2, 1),
+    ("S", 1, 1),
     ("Qs", 2, 1, 0, 1),
-    ("S", 1, 1),
     ("O", 0, 1),
     ("3", 1, 3, 0),
     ("Qs", 2, 1, 1, 2),
+    ("2", 0, 0, 1),
     ("T", 1, 1),
-    ("2", 0, 0, 1),
     ("H", 1, 3, 0),
     ("Q", 3, 1),
+    ("Qs", 3, 1, 0, 1),
+    ("S", 2, 1),
     ("Lg", 1),
-    ("S", 2, 1),
     ("O", 1, 1),
+    ("Qs", 3, 1, 1, 2),
     ("3", 0, 0, 1),
-    ("Qs", 3, 1, 0, 1),
     ("T", 2, 1),
-    ("Qs", 3, 1, 1, 2),
     ("2", 0, 1, 1),
+    ("S", 3, 1),
     ("H", 0, 0, 1),
     ("G", 0, 1),
-    ("Ld", 1),
     ("Gs", 0, 1, 0, 1),
+    ("3", 0, 1, 1),
+    ("Gs", 0, 1, 1, 2),
     ("O", 2, 1),
-    ("S", 3, 1),
-    ("Gs", 0, 1, 1, 2),
-    ("3", 0, 1, 1),
+    ("T", 3, 1),
+    ("Gs", 0, 1, 2, 3),
     ("2", 0, 2, 1),
-    ("T", 3, 1),
     ("C", 0, 1, 0, 1),
+    ("H", 0, 1, 1),
+    ("G", 1, 1),
+    ("Gs", 1, 1, 0, 1),
     ("3", 0, 2, 1),
     ("C", 0, 1, 1, 2),
-    ("Gs", 0, 1, 2, 3),
-    ("H", 0, 1, 1),
-    ("G", 1, 1),
-    ("Gs", 1, 1, 0, 3),
+    ("Gs", 1, 1, 1, 2),
     ("O", 3, 1),
+    ("Ld", 1),
     ("2", 0, 3, 1),
+    ("Gs", 1, 1, 2, 3),
     ("H", 0, 2, 1),
+    ("C", 0, 1, 2, 3),
+    ("C", 1, 1, 0, 1),
     ("G", 2, 1),
     ("Gs", 2, 1, 0, 1),
-    ("C", 1, 1, 0, 1),
     ("3", 0, 3, 1),
-    ("Gs", 2, 1, 1, 2),
-    ("C", 0, 1, 2, 3),
+    ("C", 1, 1, 1, 2),
+    ("Gs", 2, 1, 1, 3),
+    ("C", 1, 1, 2, 3),
     ("H", 0, 3, 1),
-    ("C", 1, 1, 1, 3),
     ("C", 2, 1, 0, 1),
     ("G", 3, 1),
-    ("Gs", 2, 1, 2, 3),
     ("Gs", 3, 1, 0, 1),
+    ("C", 2, 1, 1, 2),
     ("D", 0, 1),
-    ("C", 2, 1, 1, 2),
     ("Gs", 3, 1, 1, 2),
     ("D", 1, 1),
+    ("C", 2, 1, 2, 3),
+    ("Gs", 3, 1, 2, 3),
+    ("C", 3, 1, 0, 1),
     ("2", 1, 0, 1),
-    ("C", 2, 1, 2, 3),
+    ("C", 3, 1, 1, 2),
     ("2", 1, 1, 1),
-    ("Gs", 3, 1, 2, 3),
-    ("C", 3, 1, 0, 2),
+    ("C", 3, 1, 2, 3),
     ("D", 2, 1),
+    ("3", 1, 0, 1),
     ("2", 1, 2, 1),
-    ("C", 3, 1, 2, 3),
-    ("3", 1, 0, 1),
     ("3", 1, 1, 1),
     ("D", 3, 1),
     ("2", 1, 3, 1),
-    ("H", 1, 1, 1),
     ("H", 1, 0, 1),
     ("3", 1, 2, 1),
+    ("H", 1, 2, 1),
     ("3", 1, 3, 1),
-    ("H", 1, 2, 1),
+    ("H", 1, 1, 1),
     ("H", 1, 3, 1),
 ]
 
@@ -295,22 +297,22 @@
         cols = pl.ds(*GU_SENDS[n])
         return rc(GP.at[m, :, oy, :, cols], GR.at[m, :, :, cols], g_ss.at[m, n], g_rs.at[m, n], ypeer)
 
-    def compute_tile(m, j, c0, w, transposed=False):
-        xm = X[m].reshape(2 * R, DW)
+    def compute_tile(m, k, j, c0, w, transposed=False):
+        xm = X[pl.ds(m, k)].reshape(k * 2 * R, DW)
         if transposed:
             res = dot_t(xm, W1[j, pl.ds(c0, w), :]).astype(BF)
         else:
             res = dot(xm, W1[j, pl.ds(0, DW), pl.ds(c0, w)]).astype(BF)
-        GP[m, j, :, :, pl.ds(c0, w)] = res.reshape(2, R, w)
-
-    def phase_q(m, l, fresh):
+        GP[pl.ds(m, k), j, :, :, pl.ds(c0, w)] = res.reshape(k, 2, R, w)
+
+    def phase_q(m, k, l, fresh):
         for j, cnt in ((0, 4), (1, 2)):
             if fresh:
                 for i in range(cnt):
                     qkv_load(l, j * 4 + i).wait()
 
             def body(i, _):
-                compute_tile(m, j, pl.multiple_of(i * TW, TW), TW)
+                compute_tile(m, k, j, pl.multiple_of(i * TW, TW), TW)
                 return 0
             lax.fori_loop(0, cnt, body, 0)
 
@@ -318,14 +320,14 @@
         for n in range(lo, hi):
             q_copy(m, n).start()
 
-    def phase_g(m):
+    def phase_g(m, k):
         def body(i, _):
             for j in range(2):
-                compute_tile(m, j, pl.multiple_of(i * TW, TW), TW, True)
+                compute_tile(m, k, j, pl.multiple_of(i * TW, TW), TW, True)
             return 0
         lax.fori_loop(0, 5, body, 0)
         for j in range(2):
-            compute_tile(m, j, 2560, 192, True)
+            compute_tile(m, k, j, 2560, 192, True)
 
     def send_g(m, lo, hi):
         for n in range(lo, hi):
@@ -561,7 +563,7 @@
             start(wd_loads(arg[0]))
         elif op == "Q":
             m, l = arg
-            phase_q(m, l, ("q", l) not in seen)
+            phase_q(m, Q_ROWS[l], l, ("q", l) not in seen)
             seen.add(("q", l))
         elif op == "Qs":
             m, l, lo, hi = arg
@@ -592,7 +594,7 @@
             if ("g", l) not in seen:
                 wait(gu_loads(l))
                 seen.add(("g", l))
-            phase_g(m)
+            phase_g(m, G_ROWS)
         elif op == "Gs":
             m, l, lo, hi = arg
             send_g(m, lo, hi)
@@ -693,7 +695,7 @@
             out_shape=[jax.ShapeDtypeStruct(k_cache.shape, BF)] * 2,
             grid_spec=pltpu.PrefetchScalarGridSpec(
                 num_scalar_prefetch=1, grid=(L, rows // bc), in_specs=[big, big, small, small], out_specs=[big, big]),
-            compiler_params=pltpu.CompilerParams(vmem_limit_bytes=48 * 1024 * 1024),
+            compiler_params=pltpu.CompilerParams(vmem_limit_bytes=67043328),
             name="caches",
         )(start_pos, k_cache, v_cache, kn.reshape(L, rows, T, HL, HEAD_DIM), vn.reshape(L, rows, T, HL, HEAD_DIM))
         return y, k_out, v_out

time: 312 us -> 309 us (level)
  no operation moved by 1% of the time
where the time goes in v7:
time: 309 us; the launch traced here: 308 us
  Pallas kernels  302 us (98%)
  local copies, waits for them, and re-layouts  3.65 us (1%)
    pallas_call x1, Pallas kernels, device_fn(): pl.pallas_call(main_kernel, out_shape=[jax.ShapeDtypeStruct(embeds.shape,...  279 us
    pallas_call x1, Pallas kernels, device_fn(): pl.pallas_call(cache_kernel, out_shape=[jax.ShapeDtypeStruct(k_cache.shap...  23.5 us

profile of v7, /device:TPU:0, one launch (start us, length us, event | category | flops | bytes accessed | tf_op | source)
XLA Modules:
  0.0 308.4 jit_solution(355094205472316463)
XLA Ops:
  0.7 0.1 add.30
  0.7 0.7 add.26
  1.5 0.1 add.28
  1.6 0.8 fusion
  2.4 0.9 pad_maximum_fusion
  3.3 278.9 %layers.1 = (bf16[3,128,2048]{2,1,0:T(8,128)(2,1)}, bf16[2,64,24,128]{3,2,1,0:T(8,128)(2,1)}, bf16[2,64,24,128]{3,2,1,0:T(8,128)(2,1)}) custom-call(s32[128]{0:T(128)} %start_ref.3, bf16[3,128,2048]{2,1,0:T(8,128)(2,1)} %emb_ref.1, bf16[2,64,512,128]{3,2,1,0:T(8,128)(2,1)} %bitcast.6, bf16[2,64,512,128]{3,2,1,0:T(8,128)(2,1)} %bitcast.7, ...), custom_call_target="tpu_custom_call" | custom-call | tf_op jit(solution)/shard_map/layers/pallas_call | solution.py:647
  282.2 23.5 %caches.1 = (bf16[2,64,64,8,128]{4,3,2,1,0:T(8,128)(2,1)}, bf16[2,64,64,8,128]{4,3,2,1,0:T(8,128)(2,1)}) custom-call(s32[128]{0:T(128)} %start_ref.3, bf16[2,64,64,8,128]{4,3,2,1,0:T(8,128)(2,1)} %k_ref.1, bf16[2,64,64,8,128]{4,3,2,1,0:T(8,128)(2,1)} %v_ref.1, bf16[2,64,3,8,128]{4,3,2,1,0:T(8,128)(2,1)} %bitcast.10, bf16[2,64,3,8,128]{4,3,2,1,0:T(8,128)(2,1)} %bitcast.11), custom_call_target="tpu_custom_call" | custom-call | tf_op jit(solution)/shard_map/caches/pallas_call | solution.py:693
  305.7 2.7 copy.19
  (4 shorter events, 0.0 us)
